TPU v7x, 16 devices: a whole 2x2x2 slice. The times are simulated.
16 devices in a mesh: col: 4 (over z, y), row: 4 (over x, core).
Axes of the slice: x: 2, y: 2, z: 2, core: 2. Of those that a mesh axis runs over, the one named last changes fastest.
Arguments:
- mask: int32 [2048, 65536], P('row', 'col')
- user_emb: bfloat16 [2048, 64], P(('row', 'col'))
- item_emb: bfloat16 [65536, 64], P(('col', 'row'))
- queries: int32 [512], replicated
Outputs:
- output 1: bfloat16 [2048, 64], P(('row', 'col'))
- output 2: bfloat16 [65536, 64], P(('col', 'row'))
- output 3: float32 [512, 65536], P(None, ('col', 'row'))
All inputs are finite; a program needn't handle non-finite values.
Results may differ from a plain program's by a relative error of at most 0.00699888.
Values are sent between devices in bfloat16 or wider.
A program may use at most 1 GiB of HBM per device.

v0:
```python
import jax
import jax.numpy as jnp
from jax import lax
from jax.sharding import PartitionSpec as P

LAYERS = 3


def norm_block(mask_blk):
    deg_user = lax.psum(jnp.sum(mask_blk, axis=1), 'col')
    deg_item = lax.psum(jnp.sum(mask_blk, axis=0), 'row')
    inv_user = lax.rsqrt(jnp.maximum(deg_user, 1).astype(jnp.float32))
    inv_item = lax.rsqrt(jnp.maximum(deg_item, 1).astype(jnp.float32))
    return (inv_user[:, None] * mask_blk.astype(jnp.float32) * inv_item[None, :]).astype(jnp.bfloat16)


def query_scores(final_user, final_item, queries, shard_pos):
    rows_local = final_user.shape[0]
    local_idx = queries - shard_pos * rows_local
    owned = (local_idx >= 0) & (local_idx < rows_local)
    picked = jnp.take(final_user, jnp.clip(local_idx, 0, rows_local - 1), axis=0)
    picked = jnp.where(owned[:, None], picked, jnp.zeros_like(picked))
    picked = lax.psum(picked, ('row', 'col'))
    return lax.dot_general(picked, final_item, (((1,), (1,)), ((), ())), preferred_element_type=jnp.float32)


def solution(mesh):
    n_col = mesh.shape['col']
    contract_rows = (((0,), (0,)), ((), ()))

    def device_step(mask_blk, user_shard, item_shard, queries):
        norm_adj = norm_block(mask_blk)
        user_cur = user_shard
        item_cur = item_shard
        user_sum = user_shard.astype(jnp.float32)
        item_sum = item_shard.astype(jnp.float32)
        for layer_idx in range(LAYERS):
            item_panel = lax.all_gather(item_cur, 'row', axis=0, tiled=True)
            user_part = jnp.dot(norm_adj, item_panel, preferred_element_type=jnp.float32)
            user_next = lax.psum_scatter(user_part, 'col', scatter_dimension=0, tiled=True).astype(jnp.bfloat16)
            user_panel = lax.all_gather(user_cur, 'col', axis=0, tiled=True)
            item_part = lax.dot_general(norm_adj, user_panel, contract_rows, preferred_element_type=jnp.float32)
            item_next = lax.psum_scatter(item_part, 'row', scatter_dimension=0, tiled=True).astype(jnp.bfloat16)
            user_sum = user_sum + user_next.astype(jnp.float32)
            item_sum = item_sum + item_next.astype(jnp.float32)
            user_cur = user_next
            item_cur = item_next
        final_user = (user_sum / (LAYERS + 1)).astype(jnp.bfloat16)
        final_item = (item_sum / (LAYERS + 1)).astype(jnp.bfloat16)
        shard_pos = lax.axis_index('row') * n_col + lax.axis_index('col')
        scores = query_scores(final_user, final_item, queries, shard_pos)
        return final_user, final_item, scores

    return jax.shard_map(device_step, mesh=mesh, in_specs=(P('row', 'col'), P(('row', 'col'), None), P(('col', 'row'), None), P()), out_specs=(P(('row', 'col'), None), P(('col', 'row'), None), P(None, ('col', 'row'))), check_vma=False)
```

profile of v0, /device:TPU:1, one launch (start us, length us, event | category | flops | bytes accessed | tf_op | source)
XLA Modules:
  0.0 415.1 jit_solution(291000619660505946)
XLA Ops:
  7.2 0.0 all-reduce.3.cloned.1.call-start
  7.2 13.1 %fusion = (s32[512]{0:T(512)S(1)}, s32[16384]{0:T(1024)}) fusion(s32[512,16384]{1,0:T(8,128)} %param.4), kind=kLoop, calls=%fused_computation.11 | loop fusion | flops 16760320 | bytes 33622016 | tf_op jit(solution)/shard_map/reduce_sum | solution.py:10
  20.4 0.0 all-gather.4.cloned.1.call-start
  20.4 0.7 all-gather.4.cloned.1.call-update
  21.1 0.0 reduce-scatter.9.cloned.1.call-start
  21.2 6.3 %psum.21 = s32[512]{0:T(512)S(1)} all-reduce(s32[512]{0:T(512)S(1)} %get-tuple-element.3), channel_id=1, replica_groups=mesh['col'=4,'row'=4] {'col'}, use_global_device_ids=true, to_apply=%region_1.0 | all-reduce | flops 512 | bytes 4096 | tf_op jit(solution)/shard_map/psum | solution.py:10
  27.5 6.4 %all_gather.19 = bf16[512,64]{0,1:T(8,128)(2,1)S(1)} all-gather(bf16[128,64]{0,1:T(8,128)(2,1)S(1)} %copy-done.6), channel_id=1, replica_groups=mesh['col'=4,'row'=4] {'col'}, dimensions={0}, use_global_device_ids=true | all-gather | bytes 81920 | tf_op jit(solution)/shard_map/all_gather | solution.py:41
  33.9 14.8 %all-reduce.3.cloned.1.call-done = s32[16384]{0:T(1024)} async-done(((s32[16384]{0:T(1024)}), s32[16384]{0:T(1024)}) %all-reduce.3.cloned.1.call-update) | async-done | bytes 65552 | tf_op jit(solution)/shard_map/psum | solution.py:11
  48.6 0.9 convert_rsqrt_fusion
  49.5 13.1 %multiply_convert_fusion = bf16[512,16384]{1,0:T(8,128)(2,1)S(1)} fusion(s32[512,16384]{1,0:T(8,128)} %param.4, f32[16384]{0:T(1024)S(1)} %convert_rsqrt_fusion, f32[512]{0:T(512)S(1)} %convert_rsqrt_fusion.1), kind=kLoop, calls=%fused_computation.1 | loop fusion | flops 33554432 | bytes 50399232 | tf_op jit(solution)/shard_map/convert_element_type | solution.py:14
  62.7 5.7 %copy-done = bf16[512,16384]{1,0:T(8,128)(2,1)} copy-done((bf16[512,16384]{1,0:T(8,128)(2,1)}, bf16[512,16384]{1,0:T(8,128)(2,1)S(1)}, u32[]{:S(2)}) %copy-start) | copy-done | bytes 16777240
  68.4 5.0 %fusion.5 = f32[16384,64]{0,1:T(8,128)} fusion(bf16[512,64]{0,1:T(8,128)(2,1)S(1)} %all_gather.19, bf16[512,16384]{1,0:T(8,128)(2,1)S(1)} %multiply_convert_fusion), kind=kOutput, calls=%fused_computation.16 | convolution fusion | flops 1073741824 | bytes 21037056 | tf_op jit(solution)/shard_map/dot_general | solution.py:42
  73.4 0.0 reduce-scatter.7.cloned.1.call-start
  73.5 0.0 all-gather.4.cloned.1.call-done
  73.5 12.2 %fusion.1 = f32[512,64]{0,1:T(8,128)} fusion(bf16[512,16384]{1,0:T(8,128)(2,1)} %copy-done, bf16[16384,64]{0,1:T(8,128)(2,1)} %all-gather.4.cloned.1.call-done), kind=kOutput, calls=%fused_computation.12 | convolution fusion | flops 1073741824 | bytes 19005440 | tf_op jit(solution)/shard_map/dot_general | solution.py:39
  85.7 0.0 reduce-scatter.7.cloned.1.call-update
  85.7 0.0 all-gather.6.cloned.1.call-start
  85.8 29.3 %reduce-scatter.9.cloned.1.call-done = f32[4096,64]{0,1:T(8,128)} async-done(((f32[16384,64]{0,1:T(8,128)}), f32[4096,64]{0,1:T(8,128)}) %reduce-scatter.9.cloned.1.call-update) | async-done | bytes 1048592 | tf_op jit(solution)/shard_map/reduce_scatter | solution.py:43
  115.1 2.1 convert_element_type.67
  117.2 0.0 all-gather.6.cloned.1.call-update
  117.2 0.0 reduce-scatter.11.cloned.1.call-start
  117.3 20.6 %reduce-scatter.7.cloned.1.call-done = f32[128,64]{0,1:T(8,128)} async-done(((f32[512,64]{0,1:T(8,128)}), f32[128,64]{0,1:T(8,128)}) %reduce-scatter.7.cloned.1.call-update) | async-done | bytes 32784 | tf_op jit(solution)/shard_map/reduce_scatter | solution.py:40
  137.8 0.8 convert_element_type.65
  138.6 6.3 %all_gather.21 = bf16[512,64]{0,1:T(8,128)(2,1)S(1)} all-gather(bf16[128,64]{0,1:T(8,128)(2,1)S(1)} %convert_element_type.65), channel_id=1, replica_groups=mesh['col'=4,'row'=4] {'col'}, dimensions={0}, use_global_device_ids=true | all-gather | bytes 81920 | tf_op jit(solution)/shard_map/all_gather | solution.py:41
  144.9 16.3 %all-gather.6.cloned.1.call-done = bf16[16384,64]{0,1:T(8,128)(2,1)} async-done(((bf16[4096,64]{0,1:T(8,128)(2,1)}), bf16[16384,64]{0,1:T(8,128)(2,1)}) %all-gather.6.cloned.1.call-update) | async-done | bytes 2097168 | tf_op jit(solution)/shard_map/all_gather | solution.py:38
  161.2 12.2 %fusion.2 = f32[512,64]{0,1:T(8,128)} fusion(bf16[512,16384]{1,0:T(8,128)(2,1)} %copy-done, bf16[16384,64]{0,1:T(8,128)(2,1)} %all-gather.6.cloned.1.call-done), kind=kOutput, calls=%fused_computation.13 | convolution fusion | flops 1073741824 | bytes 19005440 | tf_op jit(solution)/shard_map/dot_general | solution.py:39
  173.4 0.0 reduce-scatter.13.cloned.1.call-start
  173.5 10.7 %fusion.6 = f32[16384,64]{0,1:T(8,128)} fusion(bf16[512,64]{0,1:T(8,128)(2,1)S(1)} %all_gather.21, bf16[512,16384]{1,0:T(8,128)(2,1)} %copy-done), kind=kOutput, calls=%fused_computation.17 | convolution fusion | flops 1073741824 | bytes 21037056 | tf_op jit(solution)/shard_map/dot_general | solution.py:42
  184.2 0.0 reduce-scatter.17.cloned.1.call-start
  184.3 8.8 %reduce-scatter.11.cloned.1.call-done = f32[128,64]{0,1:T(8,128)} async-done(((f32[512,64]{0,1:T(8,128)}), f32[128,64]{0,1:T(8,128)}) %reduce-scatter.11.cloned.1.call-update) | async-done | bytes 32784 | tf_op jit(solution)/shard_map/reduce_scatter | solution.py:40
  193.1 0.8 convert_element_type.68
  193.9 6.1 %all_gather.23 = bf16[512,64]{0,1:T(8,128)(2,1)S(1)} all-gather(bf16[128,64]{0,1:T(8,128)(2,1)S(1)} %convert_element_type.68), channel_id=1, replica_groups=mesh['col'=4,'row'=4] {'col'}, dimensions={0}, use_global_device_ids=true | all-gather | bytes 81920 | tf_op jit(solution)/shard_map/all_gather | solution.py:41
  200.0 10.8 %fusion.7 = f32[16384,64]{0,1:T(8,128)} fusion(bf16[512,64]{0,1:T(8,128)(2,1)S(1)} %all_gather.23, bf16[512,16384]{1,0:T(8,128)(2,1)} %copy-done), kind=kOutput, calls=%fused_computation.18 | convolution fusion | flops 1073741824 | bytes 21037056 | tf_op jit(solution)/shard_map/dot_general | solution.py:42
  210.8 0.0 all-gather.8.cloned.1.call-start
  210.9 25.2 %reduce-scatter.13.cloned.1.call-done = f32[4096,64]{0,1:T(8,128)} async-done(((f32[16384,64]{0,1:T(8,128)}), f32[4096,64]{0,1:T(8,128)}) %reduce-scatter.13.cloned.1.call-update) | async-done | bytes 1048592 | tf_op jit(solution)/shard_map/reduce_scatter | solution.py:43
  236.1 43.2 %reduce-scatter.17.cloned.1.call-done = f32[4096,64]{0,1:T(8,128)} async-done(((f32[16384,64]{0,1:T(8,128)}), f32[4096,64]{0,1:T(8,128)}) %reduce-scatter.17.cloned.1.call-update) | async-done | bytes 1048592 | tf_op jit(solution)/shard_map/reduce_scatter | solution.py:43
  279.3 2.5 multiply_convert_fusion.1
  281.9 0.3 reduce-scatter.15.cloned.1.call-start
  282.1 21.0 %all-gather.8.cloned.1.call-done = bf16[16384,64]{0,1:T(8,128)(2,1)} async-done(((bf16[4096,64]{0,1:T(8,128)(2,1)}), bf16[16384,64]{0,1:T(8,128)(2,1)}) %all-gather.8.cloned.1.call-update) | async-done | bytes 2097168 | tf_op jit(solution)/shard_map/all_gather | solution.py:38
  303.1 12.2 %fusion.3 = f32[512,64]{0,1:T(8,128)} fusion(bf16[512,16384]{1,0:T(8,128)(2,1)} %copy-done, bf16[16384,64]{0,1:T(8,128)(2,1)} %all-gather.8.cloned.1.call-done), kind=kOutput, calls=%fused_computation.14 | convolution fusion | flops 1073741824 | bytes 19005440 | tf_op jit(solution)/shard_map/dot_general | solution.py:39
  315.4 0.0 all-reduce.5.cloned.1.call-start
  315.4 19.5 %reduce-scatter.15.cloned.1.call-done = f32[128,64]{0,1:T(8,128)} async-done(((f32[512,64]{0,1:T(8,128)}), f32[128,64]{0,1:T(8,128)}) %reduce-scatter.15.cloned.1.call-update) | async-done | bytes 32784 | tf_op jit(solution)/shard_map/reduce_scatter | solution.py:40
  335.0 0.8 multiply_convert_fusion.2
  335.8 0.1 copy.7
  335.9 1.3 gather_fusion
  337.2 0.9 select_select_fusion
  338.1 65.0 %all-reduce.5.cloned.1.call-done = bf16[512,64]{1,0:T(8,128)(2,1)} async-done(((bf16[512,64]{1,0:T(8,128)(2,1)}), bf16[512,64]{1,0:T(8,128)(2,1)}) %all-reduce.5.cloned.1.call-update) | async-done | bytes 65552 | tf_op jit(solution)/shard_map/psum | solution.py:23
  403.1 5.5 %fusion.4 = f32[512,4096]{1,0:T(8,128)} fusion(bf16[512,64]{1,0:T(8,128)(2,1)} %all-reduce.5.cloned.1.call-done, bf16[4096,64]{0,1:T(8,128)(2,1)S(1)} %get-tuple-element.7), kind=kOutput, calls=%fused_computation.15 | convolution fusion | flops 268435456 | bytes 8978432 | tf_op jit(solution)/shard_map/dot_general | solution.py:24
  (28 shorter events, 0.2 us)
Async XLA Ops:
  7.2 20.3 %copy-start.6 = (bf16[128,64]{0,1:T(8,128)(2,1)S(1)}, bf16[128,64]{0,1:T(8,128)(2,1)}, u32[]{:S(2)}) copy-start(bf16[128,64]{0,1:T(8,128)(2,1)} %param.5) | copy-start | bytes 49156
  7.2 41.5 %all-reduce.3.cloned.1.call-start = ((), (), s32[]{:S(2)}) async-start(), calls=%async_computation.6 | async-start | bytes 131072 | tf_op jit(solution)/shard_map/psum | solution.py:11
  20.4 53.1 %all-gather.4.cloned.1.call-start = ((), (), s32[]{:S(2)}) async-start(), calls=%async_computation.7 | async-start | bytes 2621440 | tf_op jit(solution)/shard_map/all_gather | solution.py:38
  21.1 94.0 %reduce-scatter.9.cloned.1.call-start = ((), (), s32[]{:S(2)}) async-start(), calls=%async_computation.9 | async-start | bytes 5242880 | tf_op jit(solution)/shard_map/reduce_scatter | solution.py:43
  62.6 5.7 %copy-start = (bf16[512,16384]{1,0:T(8,128)(2,1)}, bf16[512,16384]{1,0:T(8,128)(2,1)S(1)}, u32[]{:S(2)}) copy-start(bf16[512,16384]{1,0:T(8,128)(2,1)S(1)} %multiply_convert_fusion) | copy-start | bytes 50331652
  73.4 64.4 %reduce-scatter.7.cloned.1.call-start = ((), (), s32[]{:S(2)}) async-start(), calls=%async_computation.8 | async-start | bytes 163840 | tf_op jit(solution)/shard_map/reduce_scatter | solution.py:40
  85.7 75.4 %all-gather.6.cloned.1.call-start = ((), (), s32[]{:S(2)}) async-start(), calls=%async_computation.10 | async-start | bytes 2621440 | tf_op jit(solution)/shard_map/all_gather | solution.py:38
  117.2 75.9 %reduce-scatter.11.cloned.1.call-start = ((), (), s32[]{:S(2)}) async-start(), calls=%async_computation.11 | async-start | bytes 163840 | tf_op jit(solution)/shard_map/reduce_scatter | solution.py:40
  173.4 62.7 %reduce-scatter.13.cloned.1.call-start = ((), (), s32[]{:S(2)}) async-start(), calls=%async_computation.12 | async-start | bytes 5242880 | tf_op jit(solution)/shard_map/reduce_scatter | solution.py:43
  184.2 95.1 %copy-start.1 = (f32[4096,64]{0,1:T(8,128)S(1)}, f32[4096,64]{0,1:T(8,128)}, u32[]{:S(2)}) copy-start(f32[4096,64]{0,1:T(8,128)} %reduce-scatter.9.cloned.1.call-done) | copy-start | bytes 3145732
  184.2 95.1 %copy-start.3 = (bf16[4096,64]{0,1:T(8,128)(2,1)S(1)}, bf16[4096,64]{0,1:T(8,128)(2,1)}, u32[]{:S(2)}) copy-start(bf16[4096,64]{0,1:T(8,128)(2,1)} %param.6) | copy-start | bytes 1572868
  184.2 95.0 %reduce-scatter.17.cloned.1.call-start = ((), (), s32[]{:S(2)}) async-start(), calls=%async_computation.15 | async-start | bytes 5242880 | tf_op jit(solution)/shard_map/reduce_scatter | solution.py:43
  210.8 104.6 %copy-start.8 = (s32[512]{0:T(512)S(1)}, s32[512]{0:T(512)}, u32[]{:S(2)}) copy-start(s32[512]{0:T(512)} %param.7) | copy-start | bytes 6148
  210.8 124.2 %copy-start.4 = (f32[128,64]{0,1:T(8,128)S(1)}, f32[128,64]{0,1:T(8,128)}, u32[]{:S(2)}) copy-start(f32[128,64]{0,1:T(8,128)} %reduce-scatter.7.cloned.1.call-done) | copy-start | bytes 98308
  210.8 124.2 %copy-start.5 = (f32[128,64]{0,1:T(8,128)S(1)}, f32[128,64]{0,1:T(8,128)}, u32[]{:S(2)}) copy-start(f32[128,64]{0,1:T(8,128)} %reduce-scatter.11.cloned.1.call-done) | copy-start | bytes 98308
  210.8 92.3 %all-gather.8.cloned.1.call-start = ((), (), s32[]{:S(2)}) async-start(), calls=%async_computation.13 | async-start | bytes 2621440 | tf_op jit(solution)/shard_map/all_gather | solution.py:38
  281.8 126.8 %copy-start.2 = (bf16[4096,64]{0,1:T(8,128)(2,1)}, bf16[4096,64]{0,1:T(8,128)(2,1)S(1)}, u32[]{:S(2)}) copy-start(bf16[4096,64]{0,1:T(8,128)(2,1)S(1)} %get-tuple-element.7) | copy-start | bytes 1572868
  281.9 53.1 %reduce-scatter.15.cloned.1.call-start = ((), (), s32[]{:S(2)}) async-start(), calls=%async_computation.14 | async-start | bytes 163840 | tf_op jit(solution)/shard_map/reduce_scatter | solution.py:40
  315.4 87.7 %all-reduce.5.cloned.1.call-start = ((), (), s32[]{:S(2)}) async-start(), calls=%async_computation.16 | async-start | bytes 262144 | tf_op jit(solution)/shard_map/psum | solution.py:23
  335.8 72.9 %copy-start.7 = (bf16[128,64]{0,1:T(8,128)(2,1)}, bf16[128,64]{0,1:T(8,128)(2,1)S(1)}, u32[]{:S(2)}) copy-start(bf16[128,64]{0,1:T(8,128)(2,1)S(1)} %multiply_convert_fusion.2) | copy-start | bytes 49156
Sparse Core Ops, SparseCore 0:
  20.5 28.1 all-reduce.2
  50.2 22.3 all-gather.3
  75.6 39.4 reduce-scatter.8
  117.7 20.1 reduce-scatter.6
  139.8 21.3 all-gather.5
  173.6 19.5 reduce-scatter.10
  195.6 40.3 reduce-scatter.12
  239.2 40.0 reduce-scatter.16
  282.0 21.0 all-gather.7
  315.5 19.4 reduce-scatter.14
  339.8 63.2 all-reduce.4
where the time goes:
time: 419 us; the launch traced here: 415 us
  waiting for transfers between devices  265 us (63%)
  matrix products  68.7 us (16%)
  other arithmetic  34.9 us (8%)
  blocking collectives  25 us (6%)
  between operations  14 us (3%)
  local copies, waits for them, and re-layouts  7.22 us (2%)
    reduce_scatter x3, waiting for transfers between devices, device_step(): lax.psum_scatter(item_part, 'row', scatter_dimension=0, tiled=True)  97.7 us
    psum x1, waiting for transfers between devices, query_scores(): picked = lax.psum(picked, ('row', 'col'))  65 us
    reduce_scatter x3, waiting for transfers between devices, device_step(): lax.psum_scatter(user_part, 'col', scatter_dimension=0, tiled=True)  48.9 us
    all_gather x3, waiting for transfers between devices, device_step(): item_panel = lax.all_gather(item_cur, 'row', axis=0, tiled=True)  37.3 us
    dot_general x3, matrix products, device_step(): jnp.dot(norm_adj, item_panel, preferred_element_type=jnp.float32)  36.6 us
    dot_general x3, matrix products, device_step(): lax.dot_general(norm_adj, user_panel, contract_rows, preferred_element_ty...  26.6 us
    all_gather x3, blocking collectives, device_step(): user_panel = lax.all_gather(user_cur, 'col', axis=0, tiled=True)  18.8 us
    psum x1, waiting for transfers between devices, norm_block(): deg_item = lax.psum(jnp.sum(mask_blk, axis=0), 'row')  14.8 us
  transfers between devices with their start and end apart: 11, of which 10 were waited for; matrix products, arithmetic and copies ran while one was open for 14% of the time, Pallas kernels for 0%

commit v1 on v0

v1 whole, which is shorter than its diff:
```python
import jax
import jax.numpy as jnp
from jax import lax
from jax.experimental import pallas as pl
from jax.experimental.pallas import tpu as pltpu
from jax.sharding import PartitionSpec as P

LAYERS = 3
J = 8
NSLOT = 6
F32, BF16 = jnp.float32, jnp.bfloat16


def nt(a, b):
    return lax.dot_general(a, b, (((1,), (1,)), ((), ())), preferred_element_type=F32)


def nn(a, b):
    return lax.dot_general(a, b, (((1,), (0,)), ((), ())), preferred_element_type=F32)


def remote(src, dst, send, recv, **where):
    return pltpu.make_async_remote_copy(
        src_ref=src, dst_ref=dst, send_sem=send, recv_sem=recv,
        device_id=where, device_id_type=pl.DeviceIdType.MESH)


def make_kernel(users, width, quarter, emb, shard_users, n_query):
    w = quarter // J
    rows_blk = 64
    n_rb = users // rows_blk
    lanes = w // 128

    def kern(mask, item, user, qrow, fu_out, fit_out, qt_out,
             adj, stage, item_vm, panel, ps, pk, rs, rx, isum, ut, u0t, usend, urecv, usum,
             rowacc, invu, di, di_sib, di_chip, di_x, invi, du, acc, fut, futr, fu_full,
             m_sem, i_sem, ps_s, ps_r, tx_s, tx_r, as_s, as_r, ax_s, ax_r, af_s, af_r,
             u_s, u_r, d_s, d_r, dx_s, dx_r, f_s, f_r):
        r = lax.axis_index('row')
        c = lax.axis_index('col')
        sib = r + 1 - 2 * (r % 2)
        xp = (r + 2) % 4
        dg = (sib + 2) % 4
        cols = [(c + k) % 4 for k in (1, 2, 3)]

        def mask_copy(b):
            return pltpu.make_async_copy(
                mask.at[:, pl.ds(pl.multiple_of(b * w, w), w)], stage.at[b % NSLOT], m_sem.at[b % NSLOT])

        for b in range(NSLOT):
            mask_copy(b).start()
        item_copy = pltpu.make_async_copy(item, item_vm, i_sem)
        item_copy.start()

        bar = pltpu.get_barrier_semaphore()
        for q in (sib, xp, dg):
            pl.semaphore_signal(bar, inc=1, device_id={'row': q}, device_id_type=pl.DeviceIdType.MESH)
        for q in cols:
            pl.semaphore_signal(bar, inc=1, device_id={'col': q}, device_id_type=pl.DeviceIdType.MESH)
        pl.semaphore_wait(bar, 6)

        eye = (lax.broadcasted_iota(jnp.int32, (emb, emb), 0)
               == lax.broadcasted_iota(jnp.int32, (emb, emb), 1)).astype(F32).astype(BF16)

        def ps_copy(s, j):
            return remote(ps.at[s, j], rs.at[s, j], ps_s.at[s, j], ps_r.at[s, j], row=sib)

        def tx_copy(s, j):
            return remote(pk.at[s, j, 1], rx.at[s, j], tx_s.at[s, j], tx_r.at[s, j], row=xp)

        def as_copy(s, j, q):
            return remote(panel.at[s, q, j], panel.at[s, q, j], as_s.at[s, j], as_r.at[s, j], row=sib)

        def ax_copy(s, j, q):
            return remote(panel.at[s, q, j], panel.at[s, q, j], ax_s.at[s, j], ax_r.at[s, j], row=xp)

        def af_copy(s, j, q):
            return remote(panel.at[s, q, j], panel.at[s, q, j], af_s.at[s, j], af_r.at[s, j], row=sib)

        def share_item(s, j):
            as_copy(s, j, r).start()
            ax_copy(s, j, r).start()

        item_copy.wait()

        def first_item(j, carry):
            t = nt(eye, item_vm[pl.ds(pl.multiple_of(j * w, w), w), :])
            panel[0, r, j] = t.astype(BF16)
            isum[j] = t
            share_item(0, j)
            return carry

        lax.fori_loop(0, J, first_item, 0)
        u0t[c] = nt(eye, user[...]).astype(BF16)

        def u0_copy(k, src, dst_c):
            return remote(u0t.at[src], u0t.at[src], u_s.at[0, k], u_r.at[0, k], col=dst_c)

        for k in range(3):
            u0_copy(k, c, cols[k]).start()

        rowacc[...] = jnp.zeros_like(rowacc)

        def dis_copy(q):
            return remote(di.at[q], di_sib.at[q], d_s.at[q], d_r.at[q], row=sib)

        def dix_copy(q):
            return remote(di_chip.at[q], di_x.at[q], dx_s.at[q], dx_r.at[q], row=xp)

        def chip_degree(q):
            dis_copy(q).wait_recv()
            di_chip[q] = di[q] + di_sib[q]
            dix_copy(q).start()

        for q in range(4):
            def mask_step(j, carry):
                b = q * J + j
                mask_copy(b).wait()
                slot = b % NSLOT

                def rows_step(rb, csum):
                    rows = pl.ds(pl.multiple_of(rb * rows_blk, rows_blk), rows_blk)
                    m = stage[slot, rows, :].astype(F32)
                    adj[b, rows, :] = m.astype(BF16)
                    part = m[:, :128]
                    for t in range(1, lanes):
                        part = part + m[:, t * 128:(t + 1) * 128]
                    rowacc[rows, :] = rowacc[rows, :] + part
                    for t in range(0, rows_blk, 8):
                        csum = csum + m[t:t + 8, :]
                    return csum

                csum = lax.fori_loop(0, n_rb, rows_step, jnp.zeros((8, w), F32), unroll=2)
                di[q, pl.ds(j, 1), :] = jnp.sum(csum, axis=0, keepdims=True)

                @pl.when(b + NSLOT < 4 * J)
                def _():
                    mask_copy(b + NSLOT).start()
                return carry

            lax.fori_loop(0, J, mask_step, 0)
            dis_copy(q).start()
            if q:
                chip_degree(q - 1)

        du[c] = nt(jnp.ones((8, 128), BF16), rowacc[...].astype(BF16))

        def du_copy(k, src, dst_c):
            return remote(du.at[src], du.at[src], u_s.at[4, k], u_r.at[4, k], col=dst_c)

        for k in range(3):
            du_copy(k, c, cols[k]).start()
        chip_degree(3)
        for k in range(3):
            u0_copy(k, (c + 3 - k) % 4, cols[k]).wait_recv()
        u0 = jnp.concatenate([u0t[k] for k in range(4)], axis=1)
        ut[...] = u0
        usum[...] = u0.astype(F32)
        for k in range(3):
            du_copy(k, (c + 3 - k) % 4, cols[k]).wait_recv()
        deg = ((du[0] + du[1]) + du[2]) + du[3]
        inv_row = lax.rsqrt(jnp.maximum(deg, 1.0))
        invu[...] = jnp.transpose(jnp.broadcast_to(inv_row[0:1, :], (128, users)))
        for q in range(4):
            dix_copy(q).wait_recv()
            invi[q] = lax.rsqrt(jnp.maximum(di_chip[q] + di_x[q], 1.0))

        def form(q, j):
            b = q * J + j

            def rows_step(rb, carry):
                rows = pl.ds(pl.multiple_of(rb * rows_blk, rows_blk), rows_blk)
                m = adj[b, rows, :].astype(F32)
                iu = jnp.concatenate([invu[rows, :]] * lanes, axis=1)
                adj[b, rows, :] = ((iu * m) * invi[q, pl.ds(j, 1), :]).astype(BF16)
                return carry

            lax.fori_loop(0, n_rb, rows_step, 0, unroll=2)

        def sum_send(s, j):
            ps_copy(s, j).wait_recv()
            pk[s, j, 1] = pk[s, j, 1] + rs[s, j, 1]
            tx_copy(s, j).start()

        def item_part(s):
            def step(j, carry):
                if s == 0:
                    for q in (sib, dg, r, xp):
                        form(q, j)
                u = ut[...]
                ps[s, j, 0] = nn(u, adj[sib * J + j])
                ps[s, j, 1] = nn(u, adj[dg * J + j])
                ps_copy(s, j).start()
                pk[s, j, 0] = nn(u, adj[r * J + j])
                pk[s, j, 1] = nn(u, adj[xp * J + j])

                @pl.when(j > 0)
                def _():
                    sum_send(s, j - 1)
                return carry

            lax.fori_loop(0, J, step, 0)
            sum_send(s, J - 1)

        def item_finish(s):
            def step(j, carry):
                tx_copy(s, j).wait_recv()
                v = ((pk[s, j, 0] + rs[s, j, 0]) + rx[s, j]).astype(BF16)
                total = isum[j] + v.astype(F32)
                if s < LAYERS - 1:
                    panel[s + 1, r, j] = v
                    share_item(s + 1, j)
                    isum[j] = total
                else:
                    fit_out[j] = (total / (LAYERS + 1)).astype(BF16)
                return carry

            lax.fori_loop(0, J, step, 0)

        def u_copy(s, k, src, dst_c):
            return remote(usend.at[s], urecv.at[s, src], u_s.at[s + 1, k], u_r.at[s + 1, k], col=dst_c)

        def user_part(s):
            acc[...] = jnp.zeros_like(acc)

            def add(q, j):
                acc[...] = acc[...] + nt(adj[q * J + j], panel[s, q, j])

            def step_own(j, carry):
                as_copy(s, j, sib).wait_recv()
                add(r, j)
                add(sib, j)
                return carry

            def step_far(j, carry):
                ax_copy(s, j, xp).wait_recv()
                af_copy(s, j, xp).start()
                add(xp, j)
                af_copy(s, j, dg).wait_recv()
                add(dg, j)
                return carry

            lax.fori_loop(0, J, step_own, 0)
            lax.fori_loop(0, J, step_far, 0)
            t = jnp.transpose(acc[...])
            usend[s] = t
            urecv[s, c] = t
            for k in range(3):
                u_copy(s, k, c, cols[k]).start()

        def user_finish(s):
            for k in range(3):
                u_copy(s, k, (c + 3 - k) % 4, cols[k]).wait_recv()
            v = (((urecv[s, 0] + urecv[s, 1]) + urecv[s, 2]) + urecv[s, 3]).astype(BF16)
            ut[...] = v
            usum[...] = usum[...] + v.astype(F32)

        item_part(0)
        user_part(0)
        item_finish(0)
        user_finish(0)
        item_part(1)
        user_part(1)
        item_finish(1)
        user_finish(1)
        item_part(2)
        user_part(2)
        user_finish(2)

        fu = usum[...] / (LAYERS + 1)
        fu_full[...] = jnp.transpose(fu)
        fu_out[...] = fu_full[pl.ds(pl.multiple_of(c * shard_users, shard_users), shard_users), :].astype(BF16)
        fut[r] = fu.astype(BF16)

        def fu_copy(k, q, **where):
            return remote(fut.at[q], fut.at[q], f_s.at[k], f_r.at[k], **where)

        fu_copy(0, r, row=sib).start()
        fu_copy(1, r, row=xp).start()
        fu_copy(1, xp, row=xp).wait_recv()
        fu_copy(2, xp, row=sib).start()
        fu_copy(0, sib, row=sib).wait_recv()
        fu_copy(2, dg, row=sib).wait_recv()
        qt = jnp.zeros((emb, n_query), F32)
        for q in range(4):
            ids = lax.broadcasted_iota(jnp.int32, (users, n_query), 0) + q * users
            onehot = jnp.where(ids == qrow[...], 1.0, 0.0).astype(BF16)
            qt = qt + nn(fut[q], onehot)
        qt_out[...] = qt.astype(BF16)

        item_finish(2)

        def drain(j, carry):
            for s in range(3):
                ps_copy(s, j).wait_send()
                tx_copy(s, j).wait_send()
                as_copy(s, j, r).wait_send()
                ax_copy(s, j, r).wait_send()
                af_copy(s, j, xp).wait_send()
            return carry

        lax.fori_loop(0, J, drain, 0)
        for k in range(3):
            u0_copy(k, c, cols[k]).wait_send()
            du_copy(k, c, cols[k]).wait_send()
            for s in range(3):
                u_copy(s, k, c, cols[k]).wait_send()
        for q in range(4):
            dis_copy(q).wait_send()
            dix_copy(q).wait_send()
        fu_copy(0, r, row=sib).wait_send()
        fu_copy(1, r, row=xp).wait_send()
        fu_copy(2, xp, row=sib).wait_send()

    dma = pltpu.SemaphoreType.DMA
    scratch = [
        pltpu.VMEM((4 * J, users, w), BF16),
        pltpu.VMEM((NSLOT, users, w), jnp.int32),
        pltpu.VMEM((quarter, emb), BF16),
        pltpu.VMEM((3, 4, J, emb, w), BF16),
        pltpu.VMEM((3, J, 2, emb, w), F32),
        pltpu.VMEM((3, J, 2, emb, w), F32),
        pltpu.VMEM((3, J, 2, emb, w), F32),
        pltpu.VMEM((3, J, emb, w), F32),
        pltpu.VMEM((J, emb, w), F32),
        pltpu.VMEM((emb, users), BF16),
        pltpu.VMEM((4, emb, shard_users), BF16),
        pltpu.VMEM((3, emb, users), F32),
        pltpu.VMEM((3, 4, emb, users), F32),
        pltpu.VMEM((emb, users), F32),
        pltpu.VMEM((users, 128), F32),
        pltpu.VMEM((users, 128), F32),
        pltpu.VMEM((4, J, w), F32),
        pltpu.VMEM((4, J, w), F32),
        pltpu.VMEM((4, J, w), F32),
        pltpu.VMEM((4, J, w), F32),
        pltpu.VMEM((4, J, w), F32),
        pltpu.VMEM((4, 8, users), F32),
        pltpu.VMEM((users, emb), F32),
        pltpu.VMEM((4, emb, users), BF16),
        pltpu.VMEM((8, 128), F32),
        pltpu.VMEM((users, emb), F32),
        dma((NSLOT,)), dma,
        dma((3, J)), dma((3, J)),
        dma((3, J)), dma((3, J)),
        dma((3, J)), dma((3, J)),
        dma((3, J)), dma((3, J)),
        dma((3, J)), dma((3, J)),
        dma((5, 3)), dma((5, 3)),
        dma((4,)), dma((4,)), dma((4,)), dma((4,)),
        dma((3,)), dma((3,)),
    ]
    vm, hbm = pl.BlockSpec(memory_space=pltpu.VMEM), pl.BlockSpec(memory_space=pl.ANY)
    return pl.pallas_call(
        kern,
        out_shape=(jax.ShapeDtypeStruct((shard_users, emb), BF16),
                   jax.ShapeDtypeStruct((J, emb, w), BF16),
                   jax.ShapeDtypeStruct((emb, n_query), BF16)),
        in_specs=[hbm, hbm, vm, vm],
        out_specs=(vm, vm, vm),
        scratch_shapes=scratch,
        name='propagate',
        compiler_params=pltpu.CompilerParams(
            collective_id=0, has_side_effects=True, vmem_limit_bytes=60 * 2 ** 20))


def score_kernel(qt, fit, scores, final_item):
    f = fit[0]
    scores[...] = lax.dot_general(qt[...], f, (((0,), (0,)), ((), ())), preferred_element_type=F32)
    final_item[...] = jnp.transpose(f.astype(F32)).astype(BF16)


def score(qt, fit):
    emb, n_query = qt.shape
    n, _, w = fit.shape
    return pl.pallas_call(
        score_kernel,
        grid=(n,),
        out_shape=(jax.ShapeDtypeStruct((n_query, n * w), F32), jax.ShapeDtypeStruct((n * w, emb), BF16)),
        in_specs=[pl.BlockSpec((emb, n_query), lambda j: (0, 0)), pl.BlockSpec((1, emb, w), lambda j: (j, 0, 0))],
        out_specs=(pl.BlockSpec((n_query, w), lambda j: (0, j)), pl.BlockSpec((w, emb), lambda j: (j, 0))),
        name='score',
    )(qt, fit)


def solution(mesh):
    def device_step(mask_blk, user_shard, item_shard, queries):
        users, width = mask_blk.shape
        quarter, emb = item_shard.shape
        n_query = queries.shape[0]
        call = make_kernel(users, width, quarter, emb, user_shard.shape[0], n_query)
        final_user, fit, qt = call(mask_blk, item_shard, user_shard, queries.reshape(1, n_query))
        scores, final_item = score(qt, fit)
        return final_user, final_item, scores

    return jax.shard_map(device_step, mesh=mesh, in_specs=(P('row', 'col'), P(('row', 'col'), None), P(('col', 'row'), None), P()), out_specs=(P(('row', 'col'), None), P(('col', 'row'), None), P(None, ('col', 'row'))), check_vma=False)
```

time: 419 us -> 139 us (0.33)
  waiting for transfers between devices: 265 us -> 0 us
  Pallas kernels: 0 us -> 130 us
  matrix products: 68.7 us -> 0 us
  other arithmetic: 34.9 us -> 0 us
  blocking collectives: 25 us -> 0 us
  between operations: 14 us -> 0.64 us
    reduce_scatter x6 -> x0, waiting for transfers between devices: 147 us -> none  [the longest x3 97.7 us: device_step(): lax.psum_scatter(item_part, 'row', scatter_dimension=0, tiled=True)]
    pallas_call x0 -> x2, Pallas kernels: none -> 130 us  [the longest x1 123 us: device_step(): call(mask_blk, item_shard, user_shard, queries.reshape(1, n_query))]
    psum x2 -> x0, waiting for transfers between devices: 79.7 us -> none  [the longest x1 65 us: query_scores(): picked = lax.psum(picked, ('row', 'col'))]
    dot_general x7 -> x0, matrix products: 68.7 us -> none  [the longest x3 36.6 us: device_step(): jnp.dot(norm_adj, item_panel, preferred_element_type=jnp.float32)]
    all_gather x3 -> x0, waiting for transfers between devices: 37.3 us -> none  [device_step(): item_panel = lax.all_gather(item_cur, 'row', axis=0, tiled=True)]
    convert_element_type x6 -> x0, other arithmetic: 20 us -> none  [the longest x1 13.1 us: norm_block(): (inv_user[:, None] * mask_blk.astype(jnp.float32) * inv_item[None, :]).as...]
    all_gather x3 -> x0, blocking collectives: 18.8 us -> none  [device_step(): user_panel = lax.all_gather(user_cur, 'col', axis=0, tiled=True)]
    reduce_sum x1 -> x0, other arithmetic: 13.1 us -> none  [norm_block(): deg_user = lax.psum(jnp.sum(mask_blk, axis=1), 'col')]
  transfers between devices with their start and end apart: 11 -> 0, of which waited for: 10 -> 0; matrix products, arithmetic and copies ran while one was open for 14% -> 0% of each run, Pallas kernels for 0% -> 0%
where the time goes in v1:
time: 139 us; the launch traced here: 138 us
  Pallas kernels  130 us (94%)
  local copies, waits for them, and re-layouts  7.58 us (5%)
    pallas_call x1, Pallas kernels, device_step(): call(mask_blk, item_shard, user_shard, queries.reshape(1, n_query))  123 us
    unnamed x4, local copies, waits for them, and re-layouts  7.58 us
    pallas_call x1, Pallas kernels, score(): pl.pallas_call(score_kernel, grid=(n,), out_shape=(jax.ShapeDtypeStruct((...  6.99 us

profile of v1, /device:TPU:1, one launch (start us, length us, event | category | flops | bytes accessed | tf_op | source)
XLA Modules:
  0.0 138.1 jit_solution(6970037028636183158)
XLA Ops:
  0.6 1.4 %copy.8.user = bf16[128,64]{1,0:T(8,128)(2,1)} copy(bf16[128,64]{0,1:T(8,128)(2,1)} %param.5) | data formatting | bytes 32768 | tf_op args[1]
  2.1 2.4 %copy.7.item = bf16[4096,64]{1,0:T(8,128)(2,1)} copy(bf16[4096,64]{0,1:T(8,128)(2,1)} %param.6) | data formatting | bytes 1048576 | tf_op args[2]
  4.4 122.9 %propagate.1 = (bf16[128,64]{1,0:T(8,128)(2,1)}, bf16[8,64,512]{2,1,0:T(8,128)(2,1)}, bf16[64,512]{1,0:T(8,128)(2,1)}) custom-call(s32[512,16384]{1,0:T(8,128)} %mask.1, bf16[4096,64]{1,0:T(8,128)(2,1)} %copy.7.item, bf16[128,64]{1,0:T(8,128)(2,1)} %copy.8.user, s32[1,512]{1,0:T(1,128)} %bitcast.1), custom_call_target="tpu_custom_call" | custom-call | tf_op jit(solution)/shard_map/propagate/pallas_call | solution.py:392
  127.3 1.4 %copy.9 = bf16[128,64]{0,1:T(8,128)(2,1)} copy(bf16[128,64]{1,0:T(8,128)(2,1)} %get-tuple-element.13) | data formatting | bytes 32768
  128.7 7.0 %score.1 = (f32[512,4096]{1,0:T(8,128)}, bf16[4096,64]{1,0:T(8,128)(2,1)}) custom-call(bf16[64,512]{1,0:T(8,128)(2,1)} %get-tuple-element.9.qt, bf16[8,64,512]{2,1,0:T(8,128)(2,1)} %get-tuple-element.10.fit), custom_call_target="tpu_custom_call" | custom-call | tf_op jit(solution)/shard_map/score/pallas_call | solution.py:376
  135.7 2.3 %copy.10 = bf16[4096,64]{0,1:T(8,128)(2,1)} copy(bf16[4096,64]{1,0:T(8,128)(2,1)} %get-tuple-element.14) | data formatting | bytes 1048576

commit v2 on v0

v2 whole, which is shorter than its diff:
```python
import jax
import jax.numpy as jnp
from jax import lax
from jax.experimental import pallas as pl
from jax.experimental.pallas import tpu as pltpu
from jax.sharding import PartitionSpec as P

LAYERS = 3
J = 8
NSLOT = 8
HEAD = 5
EARLY = 5
FIRST = 5
VMEM_MIB = 52
HALF = 2
F32, BF16 = jnp.float32, jnp.bfloat16


def nt(a, b):
    return lax.dot_general(a, b, (((1,), (1,)), ((), ())), preferred_element_type=F32)


def nn(a, b):
    return lax.dot_general(a, b, (((1,), (0,)), ((), ())), preferred_element_type=F32)


def remote(src, dst, send, recv, **where):
    return pltpu.make_async_remote_copy(
        src_ref=src, dst_ref=dst, send_sem=send, recv_sem=recv,
        device_id=where, device_id_type=pl.DeviceIdType.MESH)


def make_kernel(users, width, quarter, emb, shard_users, n_query):
    w = quarter // J
    piece = quarter // HALF
    rows_blk = 64
    n_rb = users // rows_blk
    lanes = w // 128

    def kern(mask, item, user, queries, fu_out, fit, q_out,
             adj, stage, panel, ps, pk, rs, rx, isum, ut, u0t, usend, urecv, usum,
             rowacc, invu, di, di_sib, di_chip, di_x, di_dg, invi, du, acc, fut, qrow,
             m_sem, i_sem, in_sem, ps_s, ps_r0, ps_r1, tx_s, tx_r, as_s, as_r, ax_s, ax_r, af_s, af_r,
             u_s, u_r, d_s, d_r, dx_s, dx_r, l_s, l_r, f_s, f_r):
        r = lax.axis_index('row')
        c = lax.axis_index('col')
        sib = r + 1 - 2 * (r % 2)
        xp = (r + 2) % 4
        dg = (sib + 2) % 4
        cols = [(c + k) % 4 for k in (1, 2, 3)]

        def over(n, body, start=0):
            def step(j, carry):
                body(j)
                return carry
            lax.fori_loop(start, n, step, 0)

        def part_of(j):
            return pl.ds(pl.multiple_of(j * w, w), w)

        def piece_of(h):
            return pl.ds(pl.multiple_of(h * piece, piece), piece)

        def mask_copy(b):
            return pltpu.make_async_copy(
                mask.at[:, pl.ds(pl.multiple_of(b * w, w), w)], stage.at[b % NSLOT], m_sem.at[b % NSLOT])

        item_copy = pltpu.make_async_copy(item, panel.at[0, r], i_sem)
        item_copy.start()
        user_copy = pltpu.make_async_copy(user, u0t.at[c], in_sem.at[0])
        user_copy.start()
        query_copy = pltpu.make_async_copy(queries, qrow, in_sem.at[1])
        query_copy.start()
        for b in range(NSLOT):
            mask_copy(b).start()

        bar = pltpu.get_barrier_semaphore()
        for q in (sib, xp, dg):
            pl.semaphore_signal(bar, inc=1, device_id={'row': q}, device_id_type=pl.DeviceIdType.MESH)
        for q in cols:
            pl.semaphore_signal(bar, inc=1, device_id={'col': q}, device_id_type=pl.DeviceIdType.MESH)

        def to_sib(src, dst, send, recv):
            return remote(src, dst, send, recv, row=sib)

        def to_xp(src, dst, send, recv):
            return remote(src, dst, send, recv, row=xp)

        def ps_near(s, j):
            return to_sib(ps.at[0, j], rs.at[s, 0, j], ps_s, ps_r0.at[s % 2])

        def ps_far(s, j):
            return to_sib(ps.at[1, j], rs.at[s, 1, j], ps_s, ps_r1.at[s % 2, j])

        def ps_near_all(s):
            return to_sib(ps.at[0], rs.at[s, 0], ps_s, ps_r0.at[s % 2])

        def ps_all(s):
            return to_sib(ps, rs.at[s], ps_s, ps_r0.at[s % 2])

        def tx_copy(s, j):
            return to_xp(pk.at[1, j], rx.at[s, j], tx_s, tx_r.at[s % 2, j])

        def tx_all(s):
            return to_xp(pk.at[1], rx.at[s], tx_s, tx_r.at[s % 2, 0])

        def as_copy(s, sl, q):
            ref = panel.at[s, q, :, sl]
            return to_sib(ref, ref, as_s.at[s % 2], as_r.at[s % 2])

        def ax_copy(s, sl, q, h):
            ref = panel.at[s, q, :, sl]
            return to_xp(ref, ref, ax_s.at[s % 2], ax_r.at[s % 2, h])

        def af_copy(s, sl, q, h):
            ref = panel.at[s, q, :, sl]
            return to_sib(ref, ref, af_s.at[s % 2], af_r.at[s % 2, h])

        whole = pl.ds(0, quarter)

        def share_far(s, j):
            ax_copy(s, part_of(j), r, j // (J // HALF)).start()

        def share_item(s, j):
            as_copy(s, part_of(j), r).start()
            share_far(s, j)

        def user_copies(kind, src, dst, slot):
            return [remote(src, dst.at[slot], u_s.at[kind], u_r.at[kind], col=q) for q in cols]

        def user_all(kind, buf):
            three = buf.at[pl.ds(0, 3)]
            return remote(three, three, u_s.at[kind], u_r.at[kind], col=cols[0])

        def dis_copy(q):
            return to_sib(di.at[q], di_sib.at[q], d_s, d_r.at[q])

        def dix_copy(q):
            return to_xp(di_chip.at[q], di_x.at[q], dx_s, dx_r.at[q])

        def chip_degree(q):
            dis_copy(q).wait_recv()
            di_chip[q] = di[q] + di_sib[q]
            dix_copy(q).start()

        rowacc[...] = jnp.zeros_like(rowacc)

        def mask_pass(q, first=0, last=J):
            def mask_step(j):
                b = q * J + j
                mask_copy(b).wait()
                slot = b % NSLOT

                def rows_step(rb, csum):
                    rows = pl.ds(pl.multiple_of(rb * rows_blk, rows_blk), rows_blk)
                    m = stage[slot, rows, :].astype(F32)
                    adj[q, rows, part_of(j)] = m.astype(BF16)
                    part = m[:, :128]
                    for t in range(1, lanes):
                        part = part + m[:, t * 128:(t + 1) * 128]
                    rowacc[rows, :] = rowacc[rows, :] + part
                    for t in range(0, rows_blk, 8):
                        csum = csum + m[t:t + 8, :]
                    return csum

                csum = lax.fori_loop(0, n_rb, rows_step, jnp.zeros((8, w), F32), unroll=2)
                di[q, pl.ds(j, 1), :] = jnp.sum(csum, axis=0, keepdims=True)

                @pl.when(b + NSLOT < 4 * J)
                def _():
                    mask_copy(b + NSLOT).start()

            over(last, mask_step, first)

        with jax.named_scope('mask_0'):
            mask_pass(0, 0, HEAD)
        with jax.named_scope('first_item'):
            item_copy.wait()
            pl.semaphore_wait(bar, 6)
            user_copy.wait()
            query_copy.wait()
            for cp in user_copies(0, u0t.at[c], u0t, c):
                cp.start()
            as_copy(0, whole, r).start()
            over(EARLY, lambda j: share_far(0, j))
        with jax.named_scope('mask_0b'):
            mask_pass(0, HEAD)
        dis_copy(0).start()
        for q in range(1, 4):
            with jax.named_scope(f'mask_{q}'):
                mask_pass(q)
            if q < 3:
                dis_copy(q).start()
            chip_degree(q - 1)

        with jax.named_scope('degrees'):
            last_di = [to_sib(di.at[3], di_sib.at[3], l_s, d_r.at[3]), to_xp(di.at[3], di_x.at[3], l_s, dx_r.at[3]),
                       remote(di.at[3], di_dg, l_s, l_r, row=dg)]
            for cp in last_di:
                cp.start()
            over(J, lambda j: share_far(0, j), EARLY)
            du[c] = nt(jnp.ones((8, 128), BF16), rowacc[...].astype(BF16))
            for cp in user_copies(4, du.at[c], du, c):
                cp.start()
            user_all(0, u0t).wait_recv()
            u0 = jnp.concatenate([u0t[k] for k in range(4)], axis=1)
            ut[...] = u0
            usum[...] = u0.astype(F32)
            with jax.named_scope('wait_di'):
                for q in range(3):
                    dix_copy(q).wait_recv()
                    invi[q] = lax.rsqrt(jnp.maximum(di_chip[q] + di_x[q], 1.0))
                for cp in last_di:
                    cp.wait_recv()
                invi[3] = lax.rsqrt(jnp.maximum((di[3] + di_sib[3]) + (di_x[3] + di_dg[...]), 1.0))
            with jax.named_scope('wait_du'):
                user_all(4, du).wait_recv()
            deg = ((du[0] + du[1]) + du[2]) + du[3]
            inv_row = lax.rsqrt(jnp.maximum(deg, 1.0))
            invu[...] = jnp.transpose(jnp.broadcast_to(inv_row[0:1, :], (128, users)))

        def form(q, j):
            def rows_step(rb, carry):
                rows = pl.ds(pl.multiple_of(rb * rows_blk, rows_blk), rows_blk)
                m = adj[q, rows, part_of(j)].astype(F32)
                iu = jnp.concatenate([invu[rows, :]] * lanes, axis=1)
                adj[q, rows, part_of(j)] = ((iu * m) * invi[q, pl.ds(j, 1), :]).astype(BF16)
                return carry

            lax.fori_loop(0, n_rb, rows_step, 0, unroll=2)

        def sum_far(s, j):
            ps_far(s, j).wait_recv()
            pk[1, j] = pk[1, j] + rs[s, 1, j]

        def item_part(s):
            def term(q, j):
                if s == 0:
                    form(q, j)
                return nn(ut[...], adj[q, :, part_of(j)])

            def step(j):
                ps[1, j] = term(dg, j)
                ps_far(s, j).start()
                pk[1, j] = term(xp, j)
                ps[0, j] = term(sib, j)
                ps_near(s, j).start()
                pk[0, j] = term(r, j)
                if s == 0:
                    sum_far(s, j)
                    tx_copy(s, j).start()
                elif s == 1:
                    @pl.when(j > 0)
                    def _():
                        sum_far(s, j - 1)
                        tx_copy(s, j - 1).start()
                else:
                    @pl.when(j > 0)
                    def _():
                        sum_far(s, j - 1)

                    @pl.when((j > 0) & (j <= FIRST))
                    def _():
                        tx_copy(s, j - 1).start()

            over(J, step)
            if s:
                sum_far(s, J - 1)
            if s == 1:
                tx_copy(s, J - 1).start()

        def item_finish(s):
            ps_near_all(s).wait_recv()

            def step(j):
                tx_copy(s, j).wait_recv()
                v = ((pk[0, j] + rs[s, 0, j]) + rx[s, j]).astype(BF16)
                before = panel[0, r, :, part_of(j)].astype(F32) if s == 0 else isum[j]
                total = before + v.astype(F32)
                if s < LAYERS - 1:
                    panel[s + 1, r, :, part_of(j)] = v
                    share_item(s + 1, j)
                    isum[j] = total
                else:
                    fit[j] = (total / (LAYERS + 1)).astype(BF16)

            over(J, step)

        def drain(s):
            ps_all(s).wait_send()
            as_copy(s, whole, r).wait_send()
            ax_copy(s, whole, r, 0).wait_send()
            af_copy(s, whole, xp, 0).wait_send()

        def user_part(s):
            def add(q, h):
                acc[...] = acc[...] + nt(adj[q, :, piece_of(h)], panel[s, q, :, piece_of(h)])

            acc[...] = jnp.zeros_like(acc)
            over(HALF, lambda h: add(r, h))
            as_copy(s, whole, sib).wait_recv()
            over(HALF, lambda h: add(sib, h))

            def far(h):
                ax_copy(s, piece_of(h), xp, h).wait_recv()
                af_copy(s, piece_of(h), xp, h).start()
                add(xp, h)
                af_copy(s, piece_of(h), dg, h).wait_recv()
                add(dg, h)

            over(HALF, far)
            t = jnp.transpose(acc[...])
            usend[s] = t
            urecv[s, c] = t
            for cp in user_copies(s + 1, usend.at[s], urecv.at[s], c):
                cp.start()

        def user_finish(s):
            user_all(s + 1, urecv.at[s]).wait_recv()
            v = (((urecv[s, 0] + urecv[s, 1]) + urecv[s, 2]) + urecv[s, 3]).astype(BF16)
            ut[...] = v
            usum[...] = usum[...] + v.astype(F32)

        for s in range(LAYERS):
            with jax.named_scope(f'item_part_{s}'):
                item_part(s)
            with jax.named_scope(f'user_part_{s}'):
                user_part(s)
            if s < LAYERS - 1:
                with jax.named_scope(f'item_finish_{s}'):
                    item_finish(s)
                    tx_all(s).wait_send()
            with jax.named_scope(f'user_finish_{s}'):
                drain(s)
                user_finish(s)

        with jax.named_scope('final_users'):
            fu = (usum[...] / (LAYERS + 1)).astype(BF16)
            for k in range(4):
                fut[r, k] = fu[:, k * shard_users:(k + 1) * shard_users]
            fu_out[...] = fut[r, c]
            cross = to_xp(fut.at[r, c], fut.at[r, c], f_s.at[0], f_r.at[0])
            cross.start()
            over(J, lambda j: tx_copy(2, j).start(), FIRST)
            own = to_sib(fut.at[r], fut.at[r], f_s.at[1], f_r.at[1])
            own.start()
            cross.wait_recv()
            spread = [remote(fut.at[xp, c], fut.at[xp, c], f_s.at[2], f_r.at[2], col=q) for q in cols]
            for cp in spread:
                cp.start()
            three = fut.at[xp, pl.ds(0, 3)]
            spread_all = remote(three, three, f_s.at[2], f_r.at[2], col=cols[0])
            spread_all.wait_recv()
            other = to_sib(fut.at[xp], fut.at[xp], f_s.at[3], f_r.at[3])
            other.start()
            own.wait_recv()
            other.wait_recv()
            qt = jnp.zeros((emb, n_query), F32)
            for q in range(4):
                ids = lax.broadcasted_iota(jnp.int32, (users, n_query), 0) + q * users
                onehot = jnp.where(ids == qrow[...], 1.0, 0.0).astype(BF16)
                qt = qt + nn(jnp.concatenate([fut[q, k] for k in range(4)], axis=1), onehot)
            q_out[...] = jnp.transpose(qt).astype(BF16)

            user_all(0, u0t).wait_send()
            user_all(4, du).wait_send()
            for s in range(3):
                user_all(s + 1, urecv.at[s]).wait_send()
            three = pl.ds(0, 3)
            to_sib(di.at[three], di_sib.at[three], d_s, d_r.at[0]).wait_send()
            to_xp(di_chip.at[three], di_x.at[three], dx_s, dx_r.at[0]).wait_send()
            to_sib(di.at[three], di_sib.at[three], l_s, d_r.at[0]).wait_send()
            cross.wait_send()
            own.wait_send()
            spread_all.wait_send()
            other.wait_send()
        with jax.named_scope('item_finish_2'):
            item_finish(2)
        with jax.named_scope('end'):
            tx_all(2).wait_send()

    dma = pltpu.SemaphoreType.DMA
    scratch = [
        pltpu.VMEM((4, users, quarter), BF16),
        pltpu.VMEM((NSLOT, users, w), jnp.int32),
        pltpu.VMEM((3, 4, emb, quarter), BF16),
        pltpu.VMEM((2, J, emb, w), F32),
        pltpu.VMEM((2, J, emb, w), F32),
        pltpu.VMEM((3, 2, J, emb, w), F32),
        pltpu.VMEM((3, J, emb, w), F32),
        pltpu.VMEM((J, emb, w), F32),
        pltpu.VMEM((emb, users), BF16),
        pltpu.VMEM((4, emb, shard_users), BF16),
        pltpu.VMEM((3, emb, users), F32),
        pltpu.VMEM((3, 4, emb, users), F32),
        pltpu.VMEM((emb, users), F32),
        pltpu.VMEM((users, 128), F32),
        pltpu.VMEM((users, 128), F32),
        pltpu.VMEM((4, J, w), F32),
        pltpu.VMEM((4, J, w), F32),
        pltpu.VMEM((4, J, w), F32),
        pltpu.VMEM((4, J, w), F32),
        pltpu.VMEM((J, w), F32),
        pltpu.VMEM((4, J, w), F32),
        pltpu.VMEM((4, 8, users), F32),
        pltpu.VMEM((users, emb), F32),
        pltpu.VMEM((4, 4, emb, shard_users), BF16),
        pltpu.VMEM((1, n_query), jnp.int32),
        dma((NSLOT,)), dma, dma((2,)),
        dma, dma((2,)), dma((2, J)),
        dma, dma((2, J)),
        dma((2,)), dma((2,)),
        dma((2,)), dma((2, HALF)),
        dma((2,)), dma((2, HALF)),
        dma((5,)), dma((5,)),
        dma, dma((4,)), dma, dma((4,)), dma, dma,
        dma((4,)), dma((4,)),
    ]
    vm, hbm = pl.BlockSpec(memory_space=pltpu.VMEM), pl.BlockSpec(memory_space=pltpu.HBM)
    return pl.pallas_call(
        kern,
        out_shape=(jax.ShapeDtypeStruct((emb, shard_users), BF16),
                   jax.ShapeDtypeStruct((J, emb, w), BF16),
                   jax.ShapeDtypeStruct((n_query, emb), BF16)),
        in_specs=[hbm, hbm, hbm, hbm],
        out_specs=(vm, vm, vm),
        scratch_shapes=scratch,
        name='propagate',
        compiler_params=pltpu.CompilerParams(
            collective_id=0, has_side_effects=True, vmem_limit_bytes=VMEM_MIB * 2 ** 20))


def score_kernel(query, fit, fu, scores, item_out, user_out, buf, s_sem, i_sem, u_sem):
    n, _, w = fit.shape
    pltpu.make_async_copy(fu, user_out, u_sem).start()

    def cols(j):
        return pl.ds(pl.multiple_of(j * w, w), w)

    def score_copy(j):
        return pltpu.make_async_copy(buf.at[j], scores.at[:, cols(j)], s_sem.at[j])

    def item_copy(j):
        return pltpu.make_async_copy(fit.at[j], item_out.at[:, cols(j)], i_sem.at[j])

    def step(j, carry):
        buf[j] = nn(query[...], fit[j])
        score_copy(j).start()
        item_copy(j).start()
        return carry

    def finish(j, carry):
        score_copy(j).wait()
        item_copy(j).wait()
        return carry

    lax.fori_loop(0, n, step, 0)
    lax.fori_loop(0, n, finish, 0)
    pltpu.make_async_copy(fu, user_out, u_sem).wait()


def score(query, fit, fu):
    n_query, emb = query.shape
    n, _, w = fit.shape
    vm, hbm = pl.BlockSpec(memory_space=pltpu.VMEM), pl.BlockSpec(memory_space=pl.ANY)
    return pl.pallas_call(
        score_kernel,
        out_shape=(jax.ShapeDtypeStruct((n_query, n * w), F32), jax.ShapeDtypeStruct((emb, n * w), BF16),
                   jax.ShapeDtypeStruct(fu.shape, BF16)),
        in_specs=[vm, vm, vm],
        out_specs=(hbm, hbm, hbm),
        scratch_shapes=[pltpu.VMEM((n, n_query, w), F32), pltpu.SemaphoreType.DMA((n,)),
                        pltpu.SemaphoreType.DMA((n,)), pltpu.SemaphoreType.DMA],
        name='score',
        compiler_params=pltpu.CompilerParams(vmem_limit_bytes=12 * 2 ** 20),
    )(query, fit, fu)


def solution(mesh):
    def device_step(mask_blk, user_shard, item_shard, queries):
        users, width = mask_blk.shape
        quarter, emb = item_shard.shape
        n_query = queries.shape[0]
        call = make_kernel(users, width, quarter, emb, user_shard.shape[0], n_query)
        fu, fit, query = call(*[pltpu.with_memory_space_constraint(a, pltpu.HBM) for a in (
            mask_blk, item_shard.T, user_shard.T, queries.reshape(1, n_query))])
        scores, final_item, final_user = score(query, fit, fu)
        return final_user.T, final_item.T, scores

    return jax.shard_map(device_step, mesh=mesh, in_specs=(P('row', 'col'), P(('row', 'col'), None), P(('col', 'row'), None), P()), out_specs=(P(('row', 'col'), None), P(('col', 'row'), None), P(None, ('col', 'row'))), check_vma=False)
```

time: 419 us -> 117 us (0.28)
  waiting for transfers between devices: 265 us -> 0 us
  Pallas kernels: 0 us -> 115 us
  matrix products: 68.7 us -> 0 us
  other arithmetic: 34.9 us -> 0 us
  blocking collectives: 25 us -> 0 us
  between operations: 14 us -> 0.64 us
  local copies, waits for them, and re-layouts: 7.22 us -> 0 us
    reduce_scatter x6 -> x0, waiting for transfers between devices: 147 us -> none  [the longest x3 97.7 us: device_step(): lax.psum_scatter(item_part, 'row', scatter_dimension=0, tiled=True)]
    pallas_call x0 -> x2, Pallas kernels: none -> 115 us  [the longest x1 112 us: device_step(): call(*[pltpu.with_memory_space_constraint(a, pltpu.HBM) for a in (mask_bl...]
    psum x2 -> x0, waiting for transfers between devices: 79.7 us -> none  [the longest x1 65 us: query_scores(): picked = lax.psum(picked, ('row', 'col'))]
    dot_general x7 -> x0, matrix products: 68.7 us -> none  [the longest x3 36.6 us: device_step(): jnp.dot(norm_adj, item_panel, preferred_element_type=jnp.float32)]
    all_gather x3 -> x0, waiting for transfers between devices: 37.3 us -> none  [device_step(): item_panel = lax.all_gather(item_cur, 'row', axis=0, tiled=True)]
    convert_element_type x6 -> x0, other arithmetic: 20 us -> none  [the longest x1 13.1 us: norm_block(): (inv_user[:, None] * mask_blk.astype(jnp.float32) * inv_item[None, :]).as...]
    all_gather x3 -> x0, blocking collectives: 18.8 us -> none  [device_step(): user_panel = lax.all_gather(user_cur, 'col', axis=0, tiled=True)]
    reduce_sum x1 -> x0, other arithmetic: 13.1 us -> none  [norm_block(): deg_user = lax.psum(jnp.sum(mask_blk, axis=1), 'col')]
  transfers between devices with their start and end apart: 11 -> 0, of which waited for: 10 -> 0; matrix products, arithmetic and copies ran while one was open for 14% -> 0% of each run, Pallas kernels for 0% -> 0%
where the time goes in v2:
time: 117 us; the launch traced here: 116 us
  Pallas kernels  115 us (98%)
    pallas_call x1, Pallas kernels, device_step(): call(*[pltpu.with_memory_space_constraint(a, pltpu.HBM) for a in (mask_bl...  112 us
    pallas_call x1, Pallas kernels, score(): pl.pallas_call(score_kernel, out_shape=(jax.ShapeDtypeStruct((n_query, n...  3.86 us

profile of v2, /device:TPU:1, one launch (start us, length us, event | category | flops | bytes accessed | tf_op | source)
XLA Modules:
  0.0 116.1 jit_solution(16834591320146455932)
XLA Ops:
  0.6 111.6 %propagate.1 = (bf16[64,128]{1,0:T(8,128)(2,1)S(1)}, bf16[8,64,512]{2,1,0:T(8,128)(2,1)S(1)}, bf16[512,64]{1,0:T(8,128)(2,1)S(1)}) custom-call(s32[512,16384]{1,0:T(8,128)} %mask.1, bf16[64,4096]{1,0:T(8,128)(2,1)} %bitcast.5, bf16[64,128]{1,0:T(8,128)(2,1)} %bitcast.6, s32[1,512]{1,0:T(1,128)} %bitcast.7), custom_call_target="tpu_custom_call" | custom-call | tf_op jit(solution)/shard_map/propagate/pallas_call | solution.py:485
  112.3 3.9 %score.1 = (f32[512,4096]{1,0:T(8,128)}, bf16[64,4096]{1,0:T(8,128)(2,1)}, bf16[64,128]{1,0:T(8,128)(2,1)}) custom-call(bf16[512,64]{1,0:T(8,128)(2,1)S(1)} %get-tuple-element.9.query, bf16[8,64,512]{2,1,0:T(8,128)(2,1)S(1)} %get-tuple-element.10.fit, bf16[64,128]{1,0:T(8,128)(2,1)S(1)} %get-tuple-element.11.fu), custom_call_target="tpu_custom_call" | custom-call | tf_op jit(solution)/shard_map/score/pallas_call | solution.py:466

commit v3 on v2

--- a/solution.py
+++ b/solution.py
@@ -8,7 +8,9 @@
 LAYERS = 3
 J = 8
 NSLOT = 8
-HEAD = 5
+HEAD = 2
+NEXT = 5
+LEAD = 2
 EARLY = 5
 FIRST = 5
 VMEM_MIB = 52
@@ -40,7 +42,7 @@
     def kern(mask, item, user, queries, fu_out, fit, q_out,
              adj, stage, panel, ps, pk, rs, rx, isum, ut, u0t, usend, urecv, usum,
              rowacc, invu, di, di_sib, di_chip, di_x, di_dg, invi, du, acc, fut, qrow,
-             m_sem, i_sem, in_sem, ps_s, ps_r0, ps_r1, tx_s, tx_r, as_s, as_r, ax_s, ax_r, af_s, af_r,
+             m_sem, i_sem, in_sem, ps_s, ps_r0, ps_r1, ps_rh, tx_s, tx_r, as_s, as_r, ax_s, ax_r, af_s, af_r,
              u_s, u_r, d_s, d_r, dx_s, dx_r, l_s, l_r, f_s, f_r):
         r = lax.axis_index('row')
         c = lax.axis_index('col')
@@ -65,8 +67,14 @@
             return pltpu.make_async_copy(
                 mask.at[:, pl.ds(pl.multiple_of(b * w, w), w)], stage.at[b % NSLOT], m_sem.at[b % NSLOT])
 
-        item_copy = pltpu.make_async_copy(item, panel.at[0, r], i_sem)
-        item_copy.start()
+        lead = LEAD * w
+
+        def item_copy(k):
+            sl = (pl.ds(0, lead), pl.ds(lead, quarter - lead))[k]
+            return pltpu.make_async_copy(item.at[:, sl], panel.at[0, r, :, sl], i_sem.at[k])
+
+        for k in range(2):
+            item_copy(k).start()
         user_copy = pltpu.make_async_copy(user, u0t.at[c], in_sem.at[0])
         user_copy.start()
         query_copy = pltpu.make_async_copy(queries, qrow, in_sem.at[1])
@@ -90,7 +98,7 @@
             return to_sib(ps.at[0, j], rs.at[s, 0, j], ps_s, ps_r0.at[s % 2])
 
         def ps_far(s, j):
-            return to_sib(ps.at[1, j], rs.at[s, 1, j], ps_s, ps_r1.at[s % 2, j])
+            return to_sib(ps.at[1, j], rs.at[s, 1, j], ps_s, ps_r1.at[j])
 
         def ps_near_all(s):
             return to_sib(ps.at[0], rs.at[s, 0], ps_s, ps_r0.at[s % 2])
@@ -99,22 +107,26 @@
             return to_sib(ps, rs.at[s], ps_s, ps_r0.at[s % 2])
 
         def tx_copy(s, j):
-            return to_xp(pk.at[1, j], rx.at[s, j], tx_s, tx_r.at[s % 2, j])
+            return to_xp(pk.at[1, j], rx.at[s, j], tx_s, tx_r.at[s % 2, j // 2])
+
+        def tx_pair(s, i):
+            two = pl.ds(2 * i, 2)
+            return to_xp(pk.at[1, two], rx.at[s, two], tx_s, tx_r.at[s % 2, i])
 
         def tx_all(s):
             return to_xp(pk.at[1], rx.at[s], tx_s, tx_r.at[s % 2, 0])
 
         def as_copy(s, sl, q):
             ref = panel.at[s, q, :, sl]
-            return to_sib(ref, ref, as_s.at[s % 2], as_r.at[s % 2])
+            return to_sib(ref, ref, as_s, as_r)
 
         def ax_copy(s, sl, q, h):
             ref = panel.at[s, q, :, sl]
-            return to_xp(ref, ref, ax_s.at[s % 2], ax_r.at[s % 2, h])
+            return to_xp(ref, ref, ax_s, ax_r.at[s % 2, h])
 
         def af_copy(s, sl, q, h):
             ref = panel.at[s, q, :, sl]
-            return to_sib(ref, ref, af_s.at[s % 2], af_r.at[s % 2, h])
+            return to_sib(ref, ref, af_s, af_r.at[h])
 
         whole = pl.ds(0, quarter)
 
@@ -126,11 +138,11 @@
             share_far(s, j)
 
         def user_copies(kind, src, dst, slot):
-            return [remote(src, dst.at[slot], u_s.at[kind], u_r.at[kind], col=q) for q in cols]
+            return [remote(src, dst.at[slot], u_s, u_r.at[kind], col=q) for q in cols]
 
         def user_all(kind, buf):
             three = buf.at[pl.ds(0, 3)]
-            return remote(three, three, u_s.at[kind], u_r.at[kind], col=cols[0])
+            return remote(three, three, u_s, u_r.at[kind], col=cols[0])
 
         def dis_copy(q):
             return to_sib(di.at[q], di_sib.at[q], d_s, d_r.at[q])
@@ -175,16 +187,19 @@
         with jax.named_scope('mask_0'):
             mask_pass(0, 0, HEAD)
         with jax.named_scope('first_item'):
-            item_copy.wait()
+            item_copy(0).wait()
             pl.semaphore_wait(bar, 6)
+            over(LEAD, lambda j: share_far(0, j))
+        with jax.named_scope('mask_0b'):
+            mask_pass(0, HEAD, NEXT)
+            item_copy(1).wait()
+            over(EARLY, lambda j: share_far(0, j), LEAD)
+            as_copy(0, whole, r).start()
             user_copy.wait()
             query_copy.wait()
             for cp in user_copies(0, u0t.at[c], u0t, c):
                 cp.start()
-            as_copy(0, whole, r).start()
-            over(EARLY, lambda j: share_far(0, j))
-        with jax.named_scope('mask_0b'):
-            mask_pass(0, HEAD)
+            mask_pass(0, NEXT)
         dis_copy(0).start()
         for q in range(1, 4):
             with jax.named_scope(f'mask_{q}'):
@@ -199,6 +214,7 @@
             for cp in last_di:
                 cp.start()
             over(J, lambda j: share_far(0, j), EARLY)
+            user_all(0, u0t).wait_send()
             du[c] = nt(jnp.ones((8, 128), BF16), rowacc[...].astype(BF16))
             for cp in user_copies(4, du.at[c], du, c):
                 cp.start()
@@ -219,12 +235,13 @@
             inv_row = lax.rsqrt(jnp.maximum(deg, 1.0))
             invu[...] = jnp.transpose(jnp.broadcast_to(inv_row[0:1, :], (128, users)))
 
-        def form(q, j):
+        def form(q, j, off=0, n=w):
             def rows_step(rb, carry):
                 rows = pl.ds(pl.multiple_of(rb * rows_blk, rows_blk), rows_blk)
-                m = adj[q, rows, part_of(j)].astype(F32)
-                iu = jnp.concatenate([invu[rows, :]] * lanes, axis=1)
-                adj[q, rows, part_of(j)] = ((iu * m) * invi[q, pl.ds(j, 1), :]).astype(BF16)
+                at = pl.ds(pl.multiple_of(j * w + off, n), n)
+                m = adj[q, rows, at].astype(F32)
+                iu = jnp.concatenate([invu[rows, :]] * (n // 128), axis=1)
+                adj[q, rows, at] = ((iu * m) * invi[q, pl.ds(j, 1), off:off + n]).astype(BF16)
                 return carry
 
             lax.fori_loop(0, n_rb, rows_step, 0, unroll=2)
@@ -232,6 +249,30 @@
         def sum_far(s, j):
             ps_far(s, j).wait_recv()
             pk[1, j] = pk[1, j] + rs[s, 1, j]
+
+        def first_part():
+            half = w // 2
+            sls = [slice(h * half, (h + 1) * half) for h in range(2)]
+            ends = [ps_rh, ps_r1.at[0]]
+
+            def half_copy(h):
+                return to_sib(ps.at[1, 0, :, sls[h]], rs.at[0, 1, 0, :, sls[h]], ps_s, ends[h])
+
+            for h in range(2):
+                form(dg, 0, h * half, half)
+                ps[1, 0, :, sls[h]] = nn(ut[...], adj[dg, :, sls[h]])
+                half_copy(h).start()
+            form(xp, 0)
+            pk[1, 0] = nn(ut[...], adj[xp, :, part_of(0)])
+            form(sib, 0)
+            ps[0, 0] = nn(ut[...], adj[sib, :, part_of(0)])
+            ps_near(0, 0).start()
+            for h in range(2):
+                half_copy(h).wait_recv()
+                pk[1, 0, :, sls[h]] = pk[1, 0, :, sls[h]] + rs[0, 1, 0, :, sls[h]]
+                to_xp(pk.at[1, 0, :, sls[h]], rx.at[0, 0, :, sls[h]], tx_s, tx_r.at[0, 0]).start()
+            form(r, 0)
+            pk[0, 0] = nn(ut[...], adj[r, :, part_of(0)])
 
         def item_part(s):
             def term(q, j):
@@ -263,7 +304,9 @@
                     def _():
                         tx_copy(s, j - 1).start()
 
-            over(J, step)
+            if s == 0:
+                first_part()
+            over(J, step, 0 if s else 1)
             if s:
                 sum_far(s, J - 1)
             if s == 1:
@@ -272,8 +315,7 @@
         def item_finish(s):
             ps_near_all(s).wait_recv()
 
-            def step(j):
-                tx_copy(s, j).wait_recv()
+            def finish(j):
                 v = ((pk[0, j] + rs[s, 0, j]) + rx[s, j]).astype(BF16)
                 before = panel[0, r, :, part_of(j)].astype(F32) if s == 0 else isum[j]
                 total = before + v.astype(F32)
@@ -284,13 +326,16 @@
                 else:
                     fit[j] = (total / (LAYERS + 1)).astype(BF16)
 
-            over(J, step)
+            def step(i):
+                tx_pair(s, i).wait_recv()
+                finish(2 * i)
+                finish(2 * i + 1)
+
+            over(J // 2, step)
 
         def drain(s):
-            ps_all(s).wait_send()
             as_copy(s, whole, r).wait_send()
             ax_copy(s, whole, r, 0).wait_send()
-            af_copy(s, whole, xp, 0).wait_send()
 
         def user_part(s):
             def add(q, h):
@@ -309,6 +354,8 @@
                 add(dg, h)
 
             over(HALF, far)
+            if s == 0:
+                user_all(4, du).wait_send()
             t = jnp.transpose(acc[...])
             usend[s] = t
             urecv[s, c] = t
@@ -317,6 +364,7 @@
 
         def user_finish(s):
             user_all(s + 1, urecv.at[s]).wait_recv()
+            user_all(s + 1, urecv.at[s]).wait_send()
             v = (((urecv[s, 0] + urecv[s, 1]) + urecv[s, 2]) + urecv[s, 3]).astype(BF16)
             ut[...] = v
             usum[...] = usum[...] + v.astype(F32)
@@ -326,12 +374,14 @@
                 item_part(s)
             with jax.named_scope(f'user_part_{s}'):
                 user_part(s)
+                drain(s)
             if s < LAYERS - 1:
                 with jax.named_scope(f'item_finish_{s}'):
                     item_finish(s)
                     tx_all(s).wait_send()
             with jax.named_scope(f'user_finish_{s}'):
-                drain(s)
+                ps_all(s).wait_send()
+                af_copy(s, whole, xp, 0).wait_send()
                 user_finish(s)
 
         with jax.named_scope('final_users'):
@@ -339,19 +389,23 @@
             for k in range(4):
                 fut[r, k] = fu[:, k * shard_users:(k + 1) * shard_users]
             fu_out[...] = fut[r, c]
-            cross = to_xp(fut.at[r, c], fut.at[r, c], f_s.at[0], f_r.at[0])
+            cross = to_xp(fut.at[r, c], fut.at[r, c], f_s, f_r.at[0])
             cross.start()
-            over(J, lambda j: tx_copy(2, j).start(), FIRST)
-            own = to_sib(fut.at[r], fut.at[r], f_s.at[1], f_r.at[1])
+            over(J - 1, lambda j: tx_copy(2, j).start(), FIRST)
+
+            @pl.when(r % 2 == 0)
+            def _():
+                tx_copy(2, J - 1).start()
+            own = to_sib(fut.at[r], fut.at[r], f_s, f_r.at[1])
             own.start()
             cross.wait_recv()
-            spread = [remote(fut.at[xp, c], fut.at[xp, c], f_s.at[2], f_r.at[2], col=q) for q in cols]
+            spread = [remote(fut.at[xp, c], fut.at[xp, c], f_s, f_r.at[2], col=q) for q in cols]
             for cp in spread:
                 cp.start()
             three = fut.at[xp, pl.ds(0, 3)]
-            spread_all = remote(three, three, f_s.at[2], f_r.at[2], col=cols[0])
+            spread_all = remote(three, three, f_s, f_r.at[2], col=cols[0])
             spread_all.wait_recv()
-            other = to_sib(fut.at[xp], fut.at[xp], f_s.at[3], f_r.at[3])
+            other = to_sib(fut.at[xp], fut.at[xp], f_s, f_r.at[3])
             other.start()
             own.wait_recv()
             other.wait_recv()
@@ -362,18 +416,15 @@
                 qt = qt + nn(jnp.concatenate([fut[q, k] for k in range(4)], axis=1), onehot)
             q_out[...] = jnp.transpose(qt).astype(BF16)
 
-            user_all(0, u0t).wait_send()
-            user_all(4, du).wait_send()
-            for s in range(3):
-                user_all(s + 1, urecv.at[s]).wait_send()
+            @pl.when(r % 2 == 1)
+            def _():
+                tx_copy(2, J - 1).start()
+
             three = pl.ds(0, 3)
             to_sib(di.at[three], di_sib.at[three], d_s, d_r.at[0]).wait_send()
             to_xp(di_chip.at[three], di_x.at[three], dx_s, dx_r.at[0]).wait_send()
             to_sib(di.at[three], di_sib.at[three], l_s, d_r.at[0]).wait_send()
-            cross.wait_send()
-            own.wait_send()
-            spread_all.wait_send()
-            other.wait_send()
+            to_sib(fut.at[three], fut.at[three], f_s, f_r.at[0]).wait_send()
         with jax.named_scope('item_finish_2'):
             item_finish(2)
         with jax.named_scope('end'):
@@ -406,15 +457,15 @@
         pltpu.VMEM((users, emb), F32),
         pltpu.VMEM((4, 4, emb, shard_users), BF16),
         pltpu.VMEM((1, n_query), jnp.int32),
-        dma((NSLOT,)), dma, dma((2,)),
-        dma, dma((2,)), dma((2, J)),
-        dma, dma((2, J)),
-        dma((2,)), dma((2,)),
-        dma((2,)), dma((2, HALF)),
-        dma((2,)), dma((2, HALF)),
-        dma((5,)), dma((5,)),
+        dma((NSLOT,)), dma((2,)), dma((2,)),
+        dma, dma((2,)), dma((J,)), dma,
+        dma, dma((2, J // 2)),
+        dma, dma,
+        dma, dma((2, HALF)),
+        dma, dma((HALF,)),
+        dma, dma((5,)),
         dma, dma((4,)), dma, dma((4,)), dma, dma,
-        dma((4,)), dma((4,)),
+        dma, dma((4,)),
     ]
     vm, hbm = pl.BlockSpec(memory_space=pltpu.VMEM), pl.BlockSpec(memory_space=pltpu.HBM)
     return pl.pallas_call(
@@ -432,31 +483,22 @@
 
 def score_kernel(query, fit, fu, scores, item_out, user_out, buf, s_sem, i_sem, u_sem):
     n, _, w = fit.shape
-    pltpu.make_async_copy(fu, user_out, u_sem).start()
+    user_copy = pltpu.make_async_copy(fu, user_out, u_sem)
+    user_copy.start()
 
     def cols(j):
         return pl.ds(pl.multiple_of(j * w, w), w)
 
-    def score_copy(j):
-        return pltpu.make_async_copy(buf.at[j], scores.at[:, cols(j)], s_sem.at[j])
-
-    def item_copy(j):
-        return pltpu.make_async_copy(fit.at[j], item_out.at[:, cols(j)], i_sem.at[j])
-
     def step(j, carry):
-        buf[j] = nn(query[...], fit[j])
-        score_copy(j).start()
-        item_copy(j).start()
+        buf[:, cols(j)] = nn(query[...], fit[j])
+        pltpu.make_async_copy(buf.at[:, cols(j)], scores.at[:, cols(j)], s_sem).start()
+        pltpu.make_async_copy(fit.at[j], item_out.at[:, cols(j)], i_sem).start()
         return carry
 
-    def finish(j, carry):
-        score_copy(j).wait()
-        item_copy(j).wait()
-        return carry
-
     lax.fori_loop(0, n, step, 0)
-    lax.fori_loop(0, n, finish, 0)
-    pltpu.make_async_copy(fu, user_out, u_sem).wait()
+    pltpu.make_async_copy(buf, scores, s_sem).wait()
+    pltpu.make_async_copy(item_out, item_out, i_sem).wait()
+    user_copy.wait()
 
 
 def score(query, fit, fu):
@@ -469,8 +511,7 @@
                    jax.ShapeDtypeStruct(fu.shape, BF16)),
         in_specs=[vm, vm, vm],
         out_specs=(hbm, hbm, hbm),
-        scratch_shapes=[pltpu.VMEM((n, n_query, w), F32), pltpu.SemaphoreType.DMA((n,)),
-                        pltpu.SemaphoreType.DMA((n,)), pltpu.SemaphoreType.DMA],
+        scratch_shapes=[pltpu.VMEM((n_query, n * w), F32)] + [pltpu.SemaphoreType.DMA] * 3,
         name='score',
         compiler_params=pltpu.CompilerParams(vmem_limit_bytes=12 * 2 ** 20),
     )(query, fit, fu)

time: 117 us -> 116 us (level)
  no operation moved by 1% of the time
where the time goes in v3:
time: 116 us
  Pallas kernels  115 us (99%)
    pallas_call x1, Pallas kernels, device_step(): call(*[pltpu.with_memory_space_constraint(a, pltpu.HBM) for a in (mask_bl...  112 us
    pallas_call x1, Pallas kernels, score(): pl.pallas_call(score_kernel, out_shape=(jax.ShapeDtypeStruct((n_query, n...  3.73 us

profile of v3, /device:TPU:1, one launch (start us, length us, event | category | flops | bytes accessed | tf_op | source)
XLA Modules:
  0.0 116.0 jit_solution(5062293049062516037)
XLA Ops:
  0.6 111.7 %propagate.1 = (bf16[64,128]{1,0:T(8,128)(2,1)S(1)}, bf16[8,64,512]{2,1,0:T(8,128)(2,1)S(1)}, bf16[512,64]{1,0:T(8,128)(2,1)S(1)}) custom-call(s32[512,16384]{1,0:T(8,128)} %mask.1, bf16[64,4096]{1,0:T(8,128)(2,1)} %bitcast.5, bf16[64,128]{1,0:T(8,128)(2,1)} %bitcast.6, s32[1,512]{1,0:T(1,128)} %bitcast.7), custom_call_target="tpu_custom_call" | custom-call | tf_op jit(solution)/shard_map/propagate/pallas_call | solution.py:526
  112.3 3.7 %score.1 = (f32[512,4096]{1,0:T(8,128)}, bf16[64,4096]{1,0:T(8,128)(2,1)}, bf16[64,128]{1,0:T(8,128)(2,1)}) custom-call(bf16[512,64]{1,0:T(8,128)(2,1)S(1)} %get-tuple-element.9.query, bf16[8,64,512]{2,1,0:T(8,128)(2,1)S(1)} %get-tuple-element.10.fit, bf16[64,128]{1,0:T(8,128)(2,1)S(1)} %get-tuple-element.11.fu), custom_call_target="tpu_custom_call" | custom-call | tf_op jit(solution)/shard_map/score/pallas_call | solution.py:508

commit v4 on v3

--- a/solution.py
+++ b/solution.py
@@ -175,7 +175,7 @@
                         csum = csum + m[t:t + 8, :]
                     return csum
 
-                csum = lax.fori_loop(0, n_rb, rows_step, jnp.zeros((8, w), F32), unroll=2)
+                csum = lax.fori_loop(0, n_rb, rows_step, jnp.zeros((8, w), F32), unroll=8)
                 di[q, pl.ds(j, 1), :] = jnp.sum(csum, axis=0, keepdims=True)
 
                 @pl.when(b + NSLOT < 4 * J)
@@ -244,7 +244,7 @@
                 adj[q, rows, at] = ((iu * m) * invi[q, pl.ds(j, 1), off:off + n]).astype(BF16)
                 return carry
 
-            lax.fori_loop(0, n_rb, rows_step, 0, unroll=2)
+            lax.fori_loop(0, n_rb, rows_step, 0, unroll=8)
 
         def sum_far(s, j):
             ps_far(s, j).wait_recv()
@@ -409,16 +409,15 @@
             other.start()
             own.wait_recv()
             other.wait_recv()
+            @pl.when(r % 2 == 1)
+            def _():
+                tx_copy(2, J - 1).start()
             qt = jnp.zeros((emb, n_query), F32)
             for q in range(4):
                 ids = lax.broadcasted_iota(jnp.int32, (users, n_query), 0) + q * users
                 onehot = jnp.where(ids == qrow[...], 1.0, 0.0).astype(BF16)
                 qt = qt + nn(jnp.concatenate([fut[q, k] for k in range(4)], axis=1), onehot)
             q_out[...] = jnp.transpose(qt).astype(BF16)
-
-            @pl.when(r % 2 == 1)
-            def _():
-                tx_copy(2, J - 1).start()
 
             three = pl.ds(0, 3)
             to_sib(di.at[three], di_sib.at[three], d_s, d_r.at[0]).wait_send()

time: 116 us -> 116 us (level)
  no operation moved by 1% of the time
where the time goes in v4:
time: 116 us
  Pallas kernels  115 us (99%)
    pallas_call x1, Pallas kernels, device_step(): call(*[pltpu.with_memory_space_constraint(a, pltpu.HBM) for a in (mask_bl...  111 us
    pallas_call x1, Pallas kernels, score(): pl.pallas_call(score_kernel, out_shape=(jax.ShapeDtypeStruct((n_query, n...  3.74 us

profile of v4, /device:TPU:1, one launch (start us, length us, event | category | flops | bytes accessed | tf_op | source)
XLA Modules:
  0.0 115.7 jit_solution(3679339218740625250)
XLA Ops:
  0.6 111.3 %propagate.1 = (bf16[64,128]{1,0:T(8,128)(2,1)S(1)}, bf16[8,64,512]{2,1,0:T(8,128)(2,1)S(1)}, bf16[512,64]{1,0:T(8,128)(2,1)S(1)}) custom-call(s32[512,16384]{1,0:T(8,128)} %mask.1, bf16[64,4096]{1,0:T(8,128)(2,1)} %bitcast.5, bf16[64,128]{1,0:T(8,128)(2,1)} %bitcast.6, s32[1,512]{1,0:T(1,128)} %bitcast.7), custom_call_target="tpu_custom_call" | custom-call | tf_op jit(solution)/shard_map/propagate/pallas_call | solution.py:525
  111.9 3.7 %score.1 = (f32[512,4096]{1,0:T(8,128)}, bf16[64,4096]{1,0:T(8,128)(2,1)}, bf16[64,128]{1,0:T(8,128)(2,1)}) custom-call(bf16[512,64]{1,0:T(8,128)(2,1)S(1)} %get-tuple-element.9.query, bf16[8,64,512]{2,1,0:T(8,128)(2,1)S(1)} %get-tuple-element.10.fit, bf16[64,128]{1,0:T(8,128)(2,1)S(1)} %get-tuple-element.11.fu), custom_call_target="tpu_custom_call" | custom-call | tf_op jit(solution)/shard_map/score/pallas_call | solution.py:507

commit v5 on v4

--- a/solution.py
+++ b/solution.py
@@ -11,7 +11,7 @@
 HEAD = 2
 NEXT = 5
 LEAD = 2
-EARLY = 5
+EARLY = 6
 FIRST = 5
 VMEM_MIB = 52
 HALF = 2
@@ -79,7 +79,7 @@
         user_copy.start()
         query_copy = pltpu.make_async_copy(queries, qrow, in_sem.at[1])
         query_copy.start()
-        for b in range(NSLOT):
+        for b in range(3):
             mask_copy(b).start()
 
         bar = pltpu.get_barrier_semaphore()
@@ -184,10 +184,14 @@
 
             over(last, mask_step, first)
 
+        for b in range(3, 5):
+            mask_copy(b).start()
         with jax.named_scope('mask_0'):
             mask_pass(0, 0, HEAD)
         with jax.named_scope('first_item'):
             item_copy(0).wait()
+            for b in range(5, NSLOT):
+                mask_copy(b).start()
             pl.semaphore_wait(bar, 6)
             over(LEAD, lambda j: share_far(0, j))
         with jax.named_scope('mask_0b'):
@@ -203,21 +207,22 @@
         dis_copy(0).start()
         for q in range(1, 4):
             with jax.named_scope(f'mask_{q}'):
-                mask_pass(q)
+                mask_pass(q, 0, J // 2)
+                chip_degree(q - 1)
+                mask_pass(q, J // 2)
             if q < 3:
                 dis_copy(q).start()
-            chip_degree(q - 1)
-
+
+        user_all(0, u0t).wait_send()
         with jax.named_scope('degrees'):
+            du[c] = nt(jnp.ones((8, 128), BF16), rowacc[...].astype(BF16))[0:1, :]
+            for cp in user_copies(4, du.at[c], du, c):
+                cp.start()
             last_di = [to_sib(di.at[3], di_sib.at[3], l_s, d_r.at[3]), to_xp(di.at[3], di_x.at[3], l_s, dx_r.at[3]),
                        remote(di.at[3], di_dg, l_s, l_r, row=dg)]
             for cp in last_di:
                 cp.start()
             over(J, lambda j: share_far(0, j), EARLY)
-            user_all(0, u0t).wait_send()
-            du[c] = nt(jnp.ones((8, 128), BF16), rowacc[...].astype(BF16))
-            for cp in user_copies(4, du.at[c], du, c):
-                cp.start()
             user_all(0, u0t).wait_recv()
             u0 = jnp.concatenate([u0t[k] for k in range(4)], axis=1)
             ut[...] = u0
@@ -233,7 +238,7 @@
                 user_all(4, du).wait_recv()
             deg = ((du[0] + du[1]) + du[2]) + du[3]
             inv_row = lax.rsqrt(jnp.maximum(deg, 1.0))
-            invu[...] = jnp.transpose(jnp.broadcast_to(inv_row[0:1, :], (128, users)))
+            invu[...] = jnp.transpose(jnp.broadcast_to(inv_row, (128, users)))
 
         def form(q, j, off=0, n=w):
             def rows_step(rb, carry):
@@ -452,7 +457,7 @@
         pltpu.VMEM((4, J, w), F32),
         pltpu.VMEM((J, w), F32),
         pltpu.VMEM((4, J, w), F32),
-        pltpu.VMEM((4, 8, users), F32),
+        pltpu.VMEM((4, 1, users), F32),
         pltpu.VMEM((users, emb), F32),
         pltpu.VMEM((4, 4, emb, shard_users), BF16),
         pltpu.VMEM((1, n_query), jnp.int32),

time: 116 us -> 116 us (level)
  no operation moved by 1% of the time
where the time goes in v5:
time: 116 us; the launch traced here: 115 us
  Pallas kernels  115 us (99%)
    pallas_call x1, Pallas kernels, device_step(): call(*[pltpu.with_memory_space_constraint(a, pltpu.HBM) for a in (mask_bl...  111 us
    pallas_call x1, Pallas kernels, score(): pl.pallas_call(score_kernel, out_shape=(jax.ShapeDtypeStruct((n_query, n...  3.74 us

profile of v5, /device:TPU:1, one launch (start us, length us, event | category | flops | bytes accessed | tf_op | source)
XLA Modules:
  0.0 115.5 jit_solution(8179303421578213688)
XLA Ops:
  0.6 111.1 %propagate.1 = (bf16[64,128]{1,0:T(8,128)(2,1)S(1)}, bf16[8,64,512]{2,1,0:T(8,128)(2,1)S(1)}, bf16[512,64]{1,0:T(8,128)(2,1)S(1)}) custom-call(s32[512,16384]{1,0:T(8,128)} %mask.1, bf16[64,4096]{1,0:T(8,128)(2,1)} %bitcast.5, bf16[64,128]{1,0:T(8,128)(2,1)} %bitcast.6, s32[1,512]{1,0:T(1,128)} %bitcast.7), custom_call_target="tpu_custom_call" | custom-call | tf_op jit(solution)/shard_map/propagate/pallas_call | solution.py:530
  111.8 3.7 %score.1 = (f32[512,4096]{1,0:T(8,128)}, bf16[64,4096]{1,0:T(8,128)(2,1)}, bf16[64,128]{1,0:T(8,128)(2,1)}) custom-call(bf16[512,64]{1,0:T(8,128)(2,1)S(1)} %get-tuple-element.9.query, bf16[8,64,512]{2,1,0:T(8,128)(2,1)S(1)} %get-tuple-element.10.fit, bf16[64,128]{1,0:T(8,128)(2,1)S(1)} %get-tuple-element.11.fu), custom_call_target="tpu_custom_call" | custom-call | tf_op jit(solution)/shard_map/score/pallas_call | solution.py:512

commit v6 on v5

--- a/solution.py
+++ b/solution.py
@@ -42,8 +42,10 @@
     def kern(mask, item, user, queries, fu_out, fit, q_out,
              adj, stage, panel, ps, pk, rs, rx, isum, ut, u0t, usend, urecv, usum,
              rowacc, invu, di, di_sib, di_chip, di_x, di_dg, invi, du, acc, fut, qrow,
-             m_sem, i_sem, in_sem, ps_s, ps_r0, ps_r1, ps_rh, tx_s, tx_r, as_s, as_r, ax_s, ax_r, af_s, af_r,
-             u_s, u_r, d_s, d_r, dx_s, dx_r, l_s, l_r, f_s, f_r):
+             m_sib, ut_sib, du_sib, invu_sib,
+             m_sem, i_sem, in_sem, ps_s, ps_r0, ps_r1, tx_s, tx_r, as_s, as_r, ax_s, ax_r, af_s, af_r,
+             u_s, u_r, d_s, d_r, dx_s, dx_r, l_s, l_r, f_s, f_r,
+             sm_s, sm_r, su_s, su_r, sd_s, sd_r):
         r = lax.axis_index('row')
         c = lax.axis_index('col')
         sib = r + 1 - 2 * (r % 2)
@@ -87,6 +89,7 @@
             pl.semaphore_signal(bar, inc=1, device_id={'row': q}, device_id_type=pl.DeviceIdType.MESH)
         for q in cols:
             pl.semaphore_signal(bar, inc=1, device_id={'col': q}, device_id_type=pl.DeviceIdType.MESH)
+            pl.semaphore_signal(bar, inc=1, device_id={'row': sib, 'col': q}, device_id_type=pl.DeviceIdType.MESH)
 
         def to_sib(src, dst, send, recv):
             return remote(src, dst, send, recv, row=sib)
@@ -192,7 +195,7 @@
             item_copy(0).wait()
             for b in range(5, NSLOT):
                 mask_copy(b).start()
-            pl.semaphore_wait(bar, 6)
+            pl.semaphore_wait(bar, 9)
             over(LEAD, lambda j: share_far(0, j))
         with jax.named_scope('mask_0b'):
             mask_pass(0, HEAD, NEXT)
@@ -214,18 +217,27 @@
                 dis_copy(q).start()
 
         user_all(0, u0t).wait_send()
+        half = w // 2
+        m_copy = to_sib(adj.at[dg, :, pl.ds(0, half)], m_sib, sm_s, sm_r)
+        ut_copy = to_sib(ut, ut_sib, su_s, su_r)
+        du_all = to_sib(du_sib, du_sib, sd_s, sd_r)
         with jax.named_scope('degrees'):
             du[c] = nt(jnp.ones((8, 128), BF16), rowacc[...].astype(BF16))[0:1, :]
             for cp in user_copies(4, du.at[c], du, c):
                 cp.start()
+            for q in cols:
+                remote(du.at[c], du_sib.at[c], sd_s, sd_r, row=sib, col=q).start()
+            to_sib(du.at[c], du_sib.at[c], sd_s, sd_r).start()
             last_di = [to_sib(di.at[3], di_sib.at[3], l_s, d_r.at[3]), to_xp(di.at[3], di_x.at[3], l_s, dx_r.at[3]),
                        remote(di.at[3], di_dg, l_s, l_r, row=dg)]
             for cp in last_di:
                 cp.start()
             over(J, lambda j: share_far(0, j), EARLY)
+            m_copy.start()
             user_all(0, u0t).wait_recv()
             u0 = jnp.concatenate([u0t[k] for k in range(4)], axis=1)
             ut[...] = u0
+            ut_copy.start()
             usum[...] = u0.astype(F32)
             with jax.named_scope('wait_di'):
                 for q in range(3):
@@ -236,9 +248,15 @@
                 invi[3] = lax.rsqrt(jnp.maximum((di[3] + di_sib[3]) + (di_x[3] + di_dg[...]), 1.0))
             with jax.named_scope('wait_du'):
                 user_all(4, du).wait_recv()
-            deg = ((du[0] + du[1]) + du[2]) + du[3]
-            inv_row = lax.rsqrt(jnp.maximum(deg, 1.0))
-            invu[...] = jnp.transpose(jnp.broadcast_to(inv_row, (128, users)))
+            def spread_degree(d):
+                deg = ((d[0] + d[1]) + d[2]) + d[3]
+                return jnp.transpose(jnp.broadcast_to(lax.rsqrt(jnp.maximum(deg, 1.0)), (128, users)))
+
+            invu[...] = spread_degree(du)
+            du_all.wait_recv()
+            invu_sib[...] = spread_degree(du_sib)
+            ut_copy.wait()
+            m_copy.wait()
 
         def form(q, j, off=0, n=w):
             def rows_step(rb, carry):
@@ -251,31 +269,39 @@
 
             lax.fori_loop(0, n_rb, rows_step, 0, unroll=8)
 
+        def form_sib():
+            def rows_step(rb, carry):
+                rows = pl.ds(pl.multiple_of(rb * rows_blk, rows_blk), rows_blk)
+                m = m_sib[rows, :].astype(F32)
+                iu = jnp.concatenate([invu_sib[rows, :]] * (half // 128), axis=1)
+                m_sib[rows, :] = ((iu * m) * invi[xp, 0:1, 0:half]).astype(BF16)
+                return carry
+
+            lax.fori_loop(0, n_rb, rows_step, 0, unroll=8)
+
         def sum_far(s, j):
             ps_far(s, j).wait_recv()
             pk[1, j] = pk[1, j] + rs[s, 1, j]
 
         def first_part():
-            half = w // 2
-            sls = [slice(h * half, (h + 1) * half) for h in range(2)]
-            ends = [ps_rh, ps_r1.at[0]]
-
-            def half_copy(h):
-                return to_sib(ps.at[1, 0, :, sls[h]], rs.at[0, 1, 0, :, sls[h]], ps_s, ends[h])
-
-            for h in range(2):
-                form(dg, 0, h * half, half)
-                ps[1, 0, :, sls[h]] = nn(ut[...], adj[dg, :, sls[h]])
-                half_copy(h).start()
-            form(xp, 0)
-            pk[1, 0] = nn(ut[...], adj[xp, :, part_of(0)])
+            lo, hi = slice(0, half), slice(half, w)
+            form(xp, 0, 0, half)
+            form_sib()
+            pk[1, 0, :, lo] = nn(ut[...], adj[xp, :, lo]) + nn(ut_sib[...], m_sib[...])
+            to_xp(pk.at[1, 0, :, lo], rx.at[0, 0, :, lo], tx_s, tx_r.at[0, 0]).start()
+            form(dg, 0, half, half)
+            ps[1, 0, :, hi] = nn(ut[...], adj[dg, :, hi])
+            hi_copy = to_sib(ps.at[1, 0, :, hi], rs.at[0, 1, 0, :, hi], ps_s, ps_r1.at[0])
+            hi_copy.start()
+            form(dg, 0, 0, half)
+            form(xp, 0, half, half)
+            pk[1, 0, :, hi] = nn(ut[...], adj[xp, :, hi])
             form(sib, 0)
             ps[0, 0] = nn(ut[...], adj[sib, :, part_of(0)])
             ps_near(0, 0).start()
-            for h in range(2):
-                half_copy(h).wait_recv()
-                pk[1, 0, :, sls[h]] = pk[1, 0, :, sls[h]] + rs[0, 1, 0, :, sls[h]]
-                to_xp(pk.at[1, 0, :, sls[h]], rx.at[0, 0, :, sls[h]], tx_s, tx_r.at[0, 0]).start()
+            hi_copy.wait_recv()
+            pk[1, 0, :, hi] = pk[1, 0, :, hi] + rs[0, 1, 0, :, hi]
+            to_xp(pk.at[1, 0, :, hi], rx.at[0, 0, :, hi], tx_s, tx_r.at[0, 0]).start()
             form(r, 0)
             pk[0, 0] = nn(ut[...], adj[r, :, part_of(0)])
 
@@ -385,7 +411,12 @@
                     item_finish(s)
                     tx_all(s).wait_send()
             with jax.named_scope(f'user_finish_{s}'):
-                ps_all(s).wait_send()
+                if s == 0:
+                    to_sib(ps.at[0], rs.at[0, 0], ps_s, ps_r0.at[0]).wait_send()
+                    to_sib(ps.at[1, pl.ds(1, J - 1)], rs.at[0, 1, pl.ds(1, J - 1)], ps_s, ps_r0.at[0]).wait_send()
+                    to_sib(ps.at[1, 0, :, pl.ds(half, half)], rs.at[0, 1, 0, :, pl.ds(half, half)], ps_s, ps_r0.at[0]).wait_send()
+                else:
+                    ps_all(s).wait_send()
                 af_copy(s, whole, xp, 0).wait_send()
                 user_finish(s)
 
@@ -428,6 +459,7 @@
             to_sib(di.at[three], di_sib.at[three], d_s, d_r.at[0]).wait_send()
             to_xp(di_chip.at[three], di_x.at[three], dx_s, dx_r.at[0]).wait_send()
             to_sib(di.at[three], di_sib.at[three], l_s, d_r.at[0]).wait_send()
+            du_all.wait_send()
             to_sib(fut.at[three], fut.at[three], f_s, f_r.at[0]).wait_send()
         with jax.named_scope('item_finish_2'):
             item_finish(2)
@@ -461,8 +493,12 @@
         pltpu.VMEM((users, emb), F32),
         pltpu.VMEM((4, 4, emb, shard_users), BF16),
         pltpu.VMEM((1, n_query), jnp.int32),
+        pltpu.VMEM((users, w // 2), BF16),
+        pltpu.VMEM((emb, users), BF16),
+        pltpu.VMEM((4, 1, users), F32),
+        pltpu.VMEM((users, 128), F32),
         dma((NSLOT,)), dma((2,)), dma((2,)),
-        dma, dma((2,)), dma((J,)), dma,
+        dma, dma((2,)), dma((J,)),
         dma, dma((2, J // 2)),
         dma, dma,
         dma, dma((2, HALF)),
@@ -470,6 +506,7 @@
         dma, dma((5,)),
         dma, dma((4,)), dma, dma((4,)), dma, dma,
         dma, dma((4,)),
+        dma, dma, dma, dma, dma, dma,
     ]
     vm, hbm = pl.BlockSpec(memory_space=pltpu.VMEM), pl.BlockSpec(memory_space=pltpu.HBM)
     return pl.pallas_call(

time: 116 us -> 115 us (level)
  no operation moved by 1% of the time
where the time goes in v6:
time: 115 us
  Pallas kernels  114 us (99%)
    pallas_call x1, Pallas kernels, device_step(): call(*[pltpu.with_memory_space_constraint(a, pltpu.HBM) for a in (mask_bl...  110 us
    pallas_call x1, Pallas kernels, score(): pl.pallas_call(score_kernel, out_shape=(jax.ShapeDtypeStruct((n_query, n...  3.74 us

profile of v6, /device:TPU:1, one launch (start us, length us, event | category | flops | bytes accessed | tf_op | source)
XLA Modules:
  0.0 114.6 jit_solution(4704121090063299905)
XLA Ops:
  0.6 110.2 %propagate.1 = (bf16[64,128]{1,0:T(8,128)(2,1)S(1)}, bf16[8,64,512]{2,1,0:T(8,128)(2,1)S(1)}, bf16[512,64]{1,0:T(8,128)(2,1)S(1)}) custom-call(s32[512,16384]{1,0:T(8,128)} %mask.1, bf16[64,4096]{1,0:T(8,128)(2,1)} %bitcast.5, bf16[64,128]{1,0:T(8,128)(2,1)} %bitcast.6, s32[1,512]{1,0:T(1,128)} %bitcast.7), custom_call_target="tpu_custom_call" | custom-call | tf_op jit(solution)/shard_map/propagate/pallas_call | solution.py:567
  110.9 3.7 %score.1 = (f32[512,4096]{1,0:T(8,128)}, bf16[64,4096]{1,0:T(8,128)(2,1)}, bf16[64,128]{1,0:T(8,128)(2,1)}) custom-call(bf16[512,64]{1,0:T(8,128)(2,1)S(1)} %get-tuple-element.9.query, bf16[8,64,512]{2,1,0:T(8,128)(2,1)S(1)} %get-tuple-element.10.fit, bf16[64,128]{1,0:T(8,128)(2,1)S(1)} %get-tuple-element.11.fu), custom_call_target="tpu_custom_call" | custom-call | tf_op jit(solution)/shard_map/score/pallas_call | solution.py:549

commit v7 on v6

--- a/solution.py
+++ b/solution.py
@@ -42,7 +42,7 @@
     def kern(mask, item, user, queries, fu_out, fit, q_out,
              adj, stage, panel, ps, pk, rs, rx, isum, ut, u0t, usend, urecv, usum,
              rowacc, invu, di, di_sib, di_chip, di_x, di_dg, invi, du, acc, fut, qrow,
-             m_sib, ut_sib, du_sib, invu_sib,
+             m_sib, ut_sib, du_sib, invu_sib, qacc,
              m_sem, i_sem, in_sem, ps_s, ps_r0, ps_r1, tx_s, tx_r, as_s, as_r, ax_s, ax_r, af_s, af_r,
              u_s, u_r, d_s, d_r, dx_s, dx_r, l_s, l_r, f_s, f_r,
              sm_s, sm_r, su_s, su_r, sd_s, sd_r):
@@ -208,19 +208,26 @@
                 cp.start()
             mask_pass(0, NEXT)
         dis_copy(0).start()
+        half = w // 2
+        m_copy = to_sib(adj.at[dg, :, pl.ds(0, half)], m_sib, sm_s, sm_r)
+        ut_copy = to_sib(ut, ut_sib, su_s, su_r)
+        du_all = to_sib(du_sib, du_sib, sd_s, sd_r)
         for q in range(1, 4):
             with jax.named_scope(f'mask_{q}'):
                 mask_pass(q, 0, J // 2)
                 chip_degree(q - 1)
+                if q == 3:
+                    m_copy.start()
+                    user_all(0, u0t).wait_recv()
+                    user_all(0, u0t).wait_send()
+                    u0 = jnp.concatenate([u0t[k] for k in range(4)], axis=1)
+                    ut[...] = u0
+                    ut_copy.start()
+                    usum[...] = u0.astype(F32)
                 mask_pass(q, J // 2)
             if q < 3:
                 dis_copy(q).start()
 
-        user_all(0, u0t).wait_send()
-        half = w // 2
-        m_copy = to_sib(adj.at[dg, :, pl.ds(0, half)], m_sib, sm_s, sm_r)
-        ut_copy = to_sib(ut, ut_sib, su_s, su_r)
-        du_all = to_sib(du_sib, du_sib, sd_s, sd_r)
         with jax.named_scope('degrees'):
             du[c] = nt(jnp.ones((8, 128), BF16), rowacc[...].astype(BF16))[0:1, :]
             for cp in user_copies(4, du.at[c], du, c):
@@ -233,12 +240,6 @@
             for cp in last_di:
                 cp.start()
             over(J, lambda j: share_far(0, j), EARLY)
-            m_copy.start()
-            user_all(0, u0t).wait_recv()
-            u0 = jnp.concatenate([u0t[k] for k in range(4)], axis=1)
-            ut[...] = u0
-            ut_copy.start()
-            usum[...] = u0.astype(F32)
             with jax.named_scope('wait_di'):
                 for q in range(3):
                     dix_copy(q).wait_recv()
@@ -444,16 +445,20 @@
             other = to_sib(fut.at[xp], fut.at[xp], f_s, f_r.at[3])
             other.start()
             own.wait_recv()
+
+            def pick(q):
+                ids = lax.broadcasted_iota(jnp.int32, (users, n_query), 0) + q * users
+                onehot = jnp.where(ids == qrow[...], 1.0, 0.0).astype(BF16)
+                return nn(jnp.concatenate([fut[q, k] for k in range(4)], axis=1), onehot)
+
+            qacc[...] = (pick(r) + pick(sib)) + pick(xp)
+
             other.wait_recv()
             @pl.when(r % 2 == 1)
             def _():
                 tx_copy(2, J - 1).start()
-            qt = jnp.zeros((emb, n_query), F32)
-            for q in range(4):
-                ids = lax.broadcasted_iota(jnp.int32, (users, n_query), 0) + q * users
-                onehot = jnp.where(ids == qrow[...], 1.0, 0.0).astype(BF16)
-                qt = qt + nn(jnp.concatenate([fut[q, k] for k in range(4)], axis=1), onehot)
-            q_out[...] = jnp.transpose(qt).astype(BF16)
+
+            q_out[...] = jnp.transpose(qacc[...] + pick(dg)).astype(BF16)
 
             three = pl.ds(0, 3)
             to_sib(di.at[three], di_sib.at[three], d_s, d_r.at[0]).wait_send()
@@ -497,6 +502,7 @@
         pltpu.VMEM((emb, users), BF16),
         pltpu.VMEM((4, 1, users), F32),
         pltpu.VMEM((users, 128), F32),
+        pltpu.VMEM((emb, n_query), F32),
         dma((NSLOT,)), dma((2,)), dma((2,)),
         dma, dma((2,)), dma((J,)),
         dma, dma((2, J // 2)),

time: 115 us -> 115 us (level)
  no operation moved by 1% of the time
where the time goes in v7:
time: 115 us
  Pallas kernels  114 us (99%)
    pallas_call x1, Pallas kernels, device_step(): call(*[pltpu.with_memory_space_constraint(a, pltpu.HBM) for a in (mask_bl...  110 us
    pallas_call x1, Pallas kernels, score(): pl.pallas_call(score_kernel, out_shape=(jax.ShapeDtypeStruct((n_query, n...  3.73 us

profile of v7, /device:TPU:1, one launch (start us, length us, event | category | flops | bytes accessed | tf_op | source)
XLA Modules:
  0.0 114.6 jit_solution(18057944921640883607)
XLA Ops:
  0.6 110.2 %propagate.1 = (bf16[64,128]{1,0:T(8,128)(2,1)S(1)}, bf16[8,64,512]{2,1,0:T(8,128)(2,1)S(1)}, bf16[512,64]{1,0:T(8,128)(2,1)S(1)}) custom-call(s32[512,16384]{1,0:T(8,128)} %mask.1, bf16[64,4096]{1,0:T(8,128)(2,1)} %bitcast.5, bf16[64,128]{1,0:T(8,128)(2,1)} %bitcast.6, s32[1,512]{1,0:T(1,128)} %bitcast.7), custom_call_target="tpu_custom_call" | custom-call | tf_op jit(solution)/shard_map/propagate/pallas_call | solution.py:573
  110.9 3.7 %score.1 = (f32[512,4096]{1,0:T(8,128)}, bf16[64,4096]{1,0:T(8,128)(2,1)}, bf16[64,128]{1,0:T(8,128)(2,1)}) custom-call(bf16[512,64]{1,0:T(8,128)(2,1)S(1)} %get-tuple-element.9.query, bf16[8,64,512]{2,1,0:T(8,128)(2,1)S(1)} %get-tuple-element.10.fit, bf16[64,128]{1,0:T(8,128)(2,1)S(1)} %get-tuple-element.11.fu), custom_call_target="tpu_custom_call" | custom-call | tf_op jit(solution)/shard_map/score/pallas_call | solution.py:555

commit v8 on v7

--- a/solution.py
+++ b/solution.py
@@ -538,7 +538,10 @@
 
     def step(j, carry):
         buf[:, cols(j)] = nn(query[...], fit[j])
-        pltpu.make_async_copy(buf.at[:, cols(j)], scores.at[:, cols(j)], s_sem).start()
+        rows = buf.shape[0] // 2
+        for k in range(2):
+            part = (pl.ds(k * rows, rows), cols(j))
+            pltpu.make_async_copy(buf.at[part], scores.at[part], s_sem).start()
         pltpu.make_async_copy(fit.at[j], item_out.at[:, cols(j)], i_sem).start()
         return carry
 

time: 115 us -> 115 us (level)
  no operation moved by 1% of the time
where the time goes in v8:
time: 115 us
  Pallas kernels  114 us (99%)
    pallas_call x1, Pallas kernels, device_step(): call(*[pltpu.with_memory_space_constraint(a, pltpu.HBM) for a in (mask_bl...  110 us
    pallas_call x1, Pallas kernels, score(): pl.pallas_call(score_kernel, out_shape=(jax.ShapeDtypeStruct((n_query, n...  3.71 us

profile of v8, /device:TPU:1, one launch (start us, length us, event | category | flops | bytes accessed | tf_op | source)
XLA Modules:
  0.0 114.6 jit_solution(15409029874573825481)
XLA Ops:
  0.6 110.2 %propagate.1 = (bf16[64,128]{1,0:T(8,128)(2,1)S(1)}, bf16[8,64,512]{2,1,0:T(8,128)(2,1)S(1)}, bf16[512,64]{1,0:T(8,128)(2,1)S(1)}) custom-call(s32[512,16384]{1,0:T(8,128)} %mask.1, bf16[64,4096]{1,0:T(8,128)(2,1)} %bitcast.5, bf16[64,128]{1,0:T(8,128)(2,1)} %bitcast.6, s32[1,512]{1,0:T(1,128)} %bitcast.7), custom_call_target="tpu_custom_call" | custom-call | tf_op jit(solution)/shard_map/propagate/pallas_call | solution.py:576
  110.9 3.7 %score.1 = (f32[512,4096]{1,0:T(8,128)}, bf16[64,4096]{1,0:T(8,128)(2,1)}, bf16[64,128]{1,0:T(8,128)(2,1)}) custom-call(bf16[512,64]{1,0:T(8,128)(2,1)S(1)} %get-tuple-element.9.query, bf16[8,64,512]{2,1,0:T(8,128)(2,1)S(1)} %get-tuple-element.10.fit, bf16[64,128]{1,0:T(8,128)(2,1)S(1)} %get-tuple-element.11.fu), custom_call_target="tpu_custom_call" | custom-call | tf_op jit(solution)/shard_map/score/pallas_call | solution.py:558
